TPU v7x, 32 devices: a whole 2x2x4 slice. The times are simulated.
32 devices in a mesh: hw: 8 (over y, x, core), head: 4 (over z).
Axes of the slice: x: 2, y: 2, z: 4, core: 2. Of those that a mesh axis runs over, the one named last changes fastest.
Arguments:
- latents: bfloat16 [8, 8, 8, 8, 5120], P('hw'), may hold values from -6 to 6
- query_weight: bfloat16 [5120, 2560], P('hw', 'head'), may hold values from -0.125 to 0.125
- key_weight: bfloat16 [5120, 2560], P('hw', 'head'), may hold values from -0.125 to 0.125
- value_weight: bfloat16 [5120, 2560], P('hw', 'head'), may hold values from -0.078125 to 0.078125
- output_weight: bfloat16 [2560, 5120], P('hw', 'head'), may hold values from -0.5 to 0.5
- query_gain: float32 [2560], P('head'), may hold values from 0.3 to 9
- key_gain: float32 [2560], P('head'), may hold values from 0.3 to 9
- frame_index: int32 [8], replicated, may hold values from 0 to 94, as said below
- row_index: int32 [32], replicated, may hold values from 0 to 286, as said below
- column_index: int32 [16], replicated, may hold values from 0 to 158, as said below
Outputs:
- attention_out: bfloat16 [8, 8, 8, 8, 5120], P('hw', None, None, None, 'head')
Inputs may be any that keep to these rules, and one draw needn't show every extreme that they name: `frame_index`: strictly increasing. `row_index`: strictly increasing. `column_index`: strictly increasing.
All inputs are finite; a program needn't handle non-finite values.
Results may differ from a plain program's by a relative error of at most 0.0075.
The roundings to bfloat16 on the way count: a program that leaves them out, or rounds other values in their place, can miss the bound.
Values may be sent and summed in bfloat16 or wider, within the bound.
A program may use at most 128 MiB of HBM per device.

v0:
```python
import math

import jax
import jax.numpy as jnp
from jax import lax
from jax.sharding import PartitionSpec as P

HEADS = 20
HD = 128
WT = 4
DEV_ROWS = 4


NORM_EPS = 0.5


def from_behind(value, axis, steps):
    count = lax.axis_size(axis)
    initial, last = (max(0, -steps), min(count, count - steps))
    return lax.ppermute(value, axis, [(source, source + steps) for source in range(initial, last)])


def freq_table(count):
    ratios = jnp.arange(count, dtype=jnp.float32) / count
    return jnp.float32(10000.0) ** (-ratios)


def rope_angles(frame_index, row_index, column_index, head_dim):
    side_pairs = head_dim // 6
    frame_pairs = head_dim // 2 - 2 * side_pairs
    frame_part = frame_index.astype(jnp.float32)[:, None] * freq_table(frame_pairs)[None, :]
    row_part = row_index.astype(jnp.float32)[:, None] * freq_table(side_pairs)[None, :]
    column_part = column_index.astype(jnp.float32)[:, None] * freq_table(side_pairs)[None, :]
    frames, rows, columns = (frame_part.shape[0], row_part.shape[0], column_part.shape[0])
    return jnp.concatenate(
        [
            jnp.broadcast_to(frame_part[:, None, None, :], (frames, rows, columns, frame_pairs)),
            jnp.broadcast_to(row_part[None, :, None, :], (frames, rows, columns, side_pairs)),
            jnp.broadcast_to(column_part[None, None, :, :], (frames, rows, columns, side_pairs)),
        ],
        axis=-1,
    )


def pair_turn(head_dim):
    source = jnp.arange(head_dim)[:, None]
    target = jnp.arange(head_dim)[None, :]
    plus = ((target % 2 == 1) & (source == target - 1)).astype(jnp.float32)
    minus = ((target % 2 == 0) & (source == target + 1)).astype(jnp.float32)
    return plus - minus


def rotate(features, angle, heads_here, head_dim):
    frames, rows, columns = (angle.shape[0], angle.shape[1], angle.shape[2])
    cosine = jnp.repeat(jnp.cos(angle), 2, axis=-1)[:, :, :, None, :]
    sine = jnp.repeat(jnp.sin(angle), 2, axis=-1)[:, :, :, None, :]
    shaped = features.reshape(frames, rows, columns, heads_here, head_dim)
    turned = jnp.dot(
        shaped.reshape(-1, head_dim), pair_turn(head_dim), precision=lax.Precision.HIGHEST
    ).reshape(shaped.shape)
    rotated = shaped * cosine + turned * sine
    return rotated.astype(jnp.bfloat16).reshape(frames, rows, columns, heads_here * head_dim)


def soft_weights(scores):
    top = jnp.max(scores, axis=-1, keepdims=True)
    raised = jnp.exp(scores - top)
    return (raised / jnp.sum(raised, axis=-1, keepdims=True)).astype(jnp.bfloat16)


def window_attend(
    queries, keys, values, first_row, first_column, total_rows, total_columns, heads_here, head_dim
):
    frames, rows, columns, width = queries.shape
    across = rows // WT
    along = columns // WT
    area = WT * WT
    scale = 1.0 / math.sqrt(head_dim)

    def tiles(array, extra):
        shaped = array.reshape(frames, across + extra, WT, along + extra, WT, heads_here, head_dim)
        return shaped.transpose(0, 1, 3, 2, 4, 5, 6).reshape(
            frames, across + extra, along + extra, area, heads_here, head_dim
        )

    query_tiles = tiles(queries, 0)
    key_tiles = tiles(keys, 2)
    value_tiles = tiles(values, 2)
    offsets = [(down, right) for down in range(3) for right in range(3)]
    key_window = jnp.concatenate(
        [key_tiles[:, down : down + across, right : right + along] for down, right in offsets],
        axis=3,
    )
    value_window = jnp.concatenate(
        [value_tiles[:, down : down + across, right : right + along] for down, right in offsets],
        axis=3,
    )
    tile_rows = first_row + jnp.arange(across)
    tile_columns = first_column + jnp.arange(along)
    inside = []
    for down, right in offsets:
        row_ok = (tile_rows + down - 1 >= 0) & (tile_rows + down - 1 < total_rows)
        column_ok = (tile_columns + right - 1 >= 0) & (tile_columns + right - 1 < total_columns)
        inside.append(row_ok[:, None] & column_ok[None, :])
    allowed = jnp.repeat(jnp.stack(inside, axis=-1), area, axis=-1)
    scores = (
        jnp.einsum(
            "fabqhd,fabkhd->fabhqk", query_tiles, key_window, preferred_element_type=jnp.float32
        )
        * scale
    )
    scores = jnp.where(allowed[None, :, :, None, None, :], scores, -jnp.inf)
    weights = soft_weights(scores)
    mixed = jnp.einsum(
        "fabhqk,fabkhd->fabqhd", weights, value_window, preferred_element_type=jnp.float32
    ).astype(jnp.bfloat16)
    mixed = mixed.reshape(frames, across, along, WT, WT, heads_here, head_dim)
    return mixed.transpose(0, 1, 3, 2, 4, 5, 6).reshape(frames, rows, columns, width)


def frame_attend(queries, keys, values, heads_here, head_dim):
    frames = queries.shape[0]
    scale = 1.0 / math.sqrt(head_dim)
    query_rows = queries.reshape(frames, -1, heads_here, head_dim)
    key_rows = keys.reshape(frames, -1, heads_here, head_dim)
    value_rows = values.reshape(frames, -1, heads_here, head_dim)
    scores = (
        jnp.einsum("fphd,gphd->phfg", query_rows, key_rows, preferred_element_type=jnp.float32)
        * scale
    )
    weights = soft_weights(scores)
    mixed = jnp.einsum(
        "phfg,gphd->fphd", weights, value_rows, preferred_element_type=jnp.float32
    ).astype(jnp.bfloat16)
    return mixed.reshape(queries.shape)


def region(stack, down, right, edge):
    rows = stack.shape[2]
    columns = stack.shape[3]
    row_start, row_stop = (rows - edge, rows) if down < 0 else (0, edge) if down > 0 else (0, rows)
    column_start, column_stop = (
        (columns - edge, columns) if right < 0 else (0, edge) if right > 0 else (0, columns)
    )
    return stack[:, :, row_start:row_stop, column_start:column_stop]


def per_device(
    latents,
    query_weight,
    key_weight,
    value_weight,
    output_weight,
    query_gain,
    key_gain,
    frame_index,
    row_index,
    column_index,
):
    frames, side, width = (latents.shape[1], latents.shape[2], latents.shape[4])
    tokens = latents.reshape(frames * side * side, width)
    head_dim = HD
    full_width = HEADS * HD
    group_width = query_weight.shape[1]
    heads_here = group_width // head_dim
    grid_columns = lax.axis_size("hw") // DEV_ROWS
    place = lax.axis_index("hw")
    grid_row = place // grid_columns
    grid_column = place % grid_columns
    tiles_side = side // WT
    query_all, key_all, value_all, output_all = (
        lax.all_gather(query_weight, "hw", axis=0, tiled=True),
        lax.all_gather(key_weight, "hw", axis=0, tiled=True),
        lax.all_gather(value_weight, "hw", axis=0, tiled=True),
        lax.all_gather(output_weight, "hw", axis=0, tiled=True),
    )
    query_lin = jnp.dot(tokens, query_all, preferred_element_type=jnp.float32)
    key_lin = jnp.dot(tokens, key_all, preferred_element_type=jnp.float32)
    value_lin = jnp.dot(tokens, value_all, preferred_element_type=jnp.float32)
    values = value_lin.astype(jnp.bfloat16)
    query_squares, key_squares = lax.psum(
        (jnp.sum(query_lin * query_lin, axis=1), jnp.sum(key_lin * key_lin, axis=1)), "head"
    )
    query_norm = query_lin * lax.rsqrt(query_squares / full_width + NORM_EPS)[:, None] * query_gain
    key_norm = key_lin * lax.rsqrt(key_squares / full_width + NORM_EPS)[:, None] * key_gain
    rows_here = lax.dynamic_slice_in_dim(row_index, grid_row * side, side)
    columns_here = lax.dynamic_slice_in_dim(column_index, grid_column * side, side)
    angle = rope_angles(frame_index, rows_here, columns_here, head_dim)
    queries_grid = rotate(query_norm, angle, heads_here, head_dim)
    keys_grid = rotate(key_norm, angle, heads_here, head_dim)
    values_grid = values.reshape(frames, side, side, group_width)
    stack = jnp.stack([keys_grid, values_grid])
    received = {}
    for down in (-1, 0, 1):
        for right in (-1, 0, 1):
            if down != 0 or right != 0:
                received[down, right] = from_behind(
                    region(stack, down, right, WT), "hw", -(down * grid_columns + right)
                )
    received[0, 0] = stack
    bands = [
        jnp.concatenate([received[down, right] for right in (-1, 0, 1)], axis=3)
        for down in (-1, 0, 1)
    ]
    padded = jnp.concatenate(bands, axis=2)
    spatial = window_attend(
        queries_grid,
        padded[0],
        padded[1],
        grid_row * tiles_side,
        grid_column * tiles_side,
        DEV_ROWS * tiles_side,
        grid_columns * tiles_side,
        heads_here,
        head_dim,
    )
    mixed = frame_attend(queries_grid, keys_grid, spatial, heads_here, head_dim)
    gathered = lax.all_gather(mixed.reshape(-1, group_width), "head", axis=1, tiled=True)
    result = jnp.dot(gathered, output_all, preferred_element_type=jnp.float32)
    return result.astype(jnp.bfloat16).reshape(1, frames, side, side, output_weight.shape[1])


def solution(mesh):
    placed = (
        P("hw", None, None, None, None),
        P("hw", "head"),
        P("hw", "head"),
        P("hw", "head"),
        P("hw", "head"),
        P("head"),
        P("head"),
        P(),
        P(),
        P(),
    )
    return jax.shard_map(
        per_device,
        mesh=mesh,
        in_specs=placed,
        out_specs=P("hw", None, None, None, "head"),
        check_vma=False,
    )
```

profile of v0, /device:TPU:5, one launch (start us, length us, event | category | flops | bytes accessed | tf_op | source)
XLA Modules:
  0.0 363.0 jit_solution(12764319904569927648)
XLA Ops:
  15.4 2.8 copy.29
  21.3 2.8 copy.31
  24.1 33.0 %all-gather.6.cloned.1.call-done = bf16[5120,640]{1,0:T(8,128)(2,1)} async-done(((bf16[640,640]{1,0:T(8,128)(2,1)}), bf16[5120,640]{1,0:T(8,128)(2,1)}) %all-gather.6.cloned.1.call-update) | async-done | bytes 6553616 | tf_op jit(solution)/shard_map/all_gather | solution.py:173
  57.1 8.2 %multiply_reduce_fusion.1 = (f32[512]{0:T(512)S(1)}, f32[512,640]{1,0:T(8,128)S(1)}) fusion(bf16[512,5120]{1,0:T(8,128)(2,1)} %bitcast.100, bf16[5120,640]{1,0:T(8,128)(2,1)} %all-gather.6.cloned.1.call-done), kind=kOutput, calls=%fused_computation.41 | convolution fusion | flops 3356098048 | bytes 13109248 | tf_op jit(solution)/shard_map/dot_general | solution.py:178
  65.3 40.2 %all-gather.10.cloned.1.call-done = bf16[5120,640]{1,0:T(8,128)(2,1)} async-done(((bf16[640,640]{1,0:T(8,128)(2,1)}), bf16[5120,640]{1,0:T(8,128)(2,1)}) %all-gather.10.cloned.1.call-update) | async-done | bytes 6553616 | tf_op jit(solution)/shard_map/all_gather | solution.py:172
  105.5 9.7 %multiply_reduce_fusion = (f32[512]{0:T(512)S(1)}, f32[512,640]{1,0:T(8,128)}) fusion(bf16[512,5120]{1,0:T(8,128)(2,1)} %bitcast.101, bf16[5120,640]{1,0:T(8,128)(2,1)} %all-gather.10.cloned.1.call-done), kind=kOutput, calls=%fused_computation.39 | convolution fusion | flops 3356098048 | bytes 13109248 | tf_op jit(solution)/shard_map/dot_general | solution.py:177
  115.2 9.8 %all-reduce = (f32[512]{0:T(512)S(1)}, f32[512]{0:T(512)S(1)}) all-reduce(f32[512]{0:T(512)S(1)} %get-tuple-element.30, f32[512]{0:T(512)S(1)} %get-tuple-element.32), channel_id=1, replica_groups=mesh['hw'=8,'head'=4] {'head'}, use_global_device_ids=true, to_apply=%region_1.2 | all-reduce | flops 1024 | bytes 8192 | tf_op jit(solution)/shard_map/psum | solution.py:181
  126.5 27.5 %all-gather.8.cloned.1.call-done = bf16[5120,640]{1,0:T(8,128)(2,1)} async-done(((bf16[640,640]{1,0:T(8,128)(2,1)}), bf16[5120,640]{1,0:T(8,128)(2,1)}) %all-gather.8.cloned.1.call-update) | async-done | bytes 6553616 | tf_op jit(solution)/shard_map/all_gather | solution.py:174
  153.9 8.6 %convolution_convert_fusion.2 = bf16[512,640]{1,0:T(8,128)(2,1)S(1)} fusion(bf16[512,5120]{1,0:T(8,128)(2,1)} %bitcast.102, bf16[5120,640]{1,0:T(8,128)(2,1)} %all-gather.8.cloned.1.call-done), kind=kOutput, calls=%fused_computation.32 | convolution fusion | flops 3355770880 | bytes 12451840 | tf_op jit(solution)/shard_map/dot_general | solution.py:179
  168.2 2.8 collective-permute-start.5
  178.1 3.2 collective-permute-done
  181.3 8.0 %collective-permute-start.4 = (bf16[2,8,8,4,640]{4,3,2,1,0:T(4,128)(2,1)}, bf16[2,8,8,4,640]{4,3,2,1,0:T(4,128)(2,1)}, u32[]{:S(2)}, u32[]{:S(2)}) collective-permute-start(bf16[2,8,8,4,640]{4,3,2,1,0:T(4,128)(2,1)} %get-tuple-element.16), channel_id=1, source_target_pairs={{4,0},{8,4},{12,8},{16,12},{20,16},{24,20},{28,24},{5,1},{9,5},{13... | collective-permute-start | bytes 1966088 | tf_op jit(solution)/shard_map/ppermute | solution.py:20
  193.1 2.6 collective-permute-start.7
  197.6 3.3 fusion.56
  200.9 46.0 %collective-permute-done.7 = bf16[2,8,4,4,640]{4,3,2,1,0:T(4,128)(2,1)} collective-permute-done((bf16[2,8,4,4,640]{4,3,2,1,0:T(4,128)(2,1)}, bf16[2,8,4,4,640]{4,3,2,1,0:T(4,128)(2,1)}, u32[]{:S(2)}, u32[]{:S(2)}) %collective-permute-start.7) | collective-permute-done | bytes 327712 | tf_op jit(solution)/shard_map/ppermute | solution.py:20
  246.8 5.9 %maximum_maximum_fusion = bf16[2,8,16,16,640]{4,3,2,1,0:T(8,128)(2,1)S(1)} fusion(bf16[2,8,4,4,640]{4,3,2,1,0:T(4,128)(2,1)} %collective-permute-done.7, bf16[2,8,4,8,640]{4,3,2,1,0:T(8,128)(2,1)} %collective-permute-done.6, bf16[2,8,4,4,640]{4,3,2,1,0:T(4,128)(2,1)} %copy-done.3, bf16[2,8,8,4,640]{4,3,2,1,0:T(4,128)(2,1)} %collective-permute-done.4, ...), kind=kLoop, calls=%fused_computation.2 | loop fusion | flops 52428800 | bytes 10485760 | tf_op jit(solution)/shard_map/concatenate | solution.py:205
  254.9 4.2 %reshape_squeeze.7 = bf16[8,4,4,4,4,5,128]{6,5,4,3,2,1,0:T(8,128)(2,1)} reshape(bf16[1,8,16,16,640]{4,3,2,1,0:T(8,128)(2,1)S(1)} %get-tuple-element.7) | data formatting | bytes 5242880 | tf_op jit(solution)/shard_map/reshape;squeeze | solution.py:81
  259.1 3.7 %copy.34 = bf16[8,4,4,4,4,5,128]{6,4,3,5,2,1,0:T(4,128)(2,1)S(1)} copy(bf16[8,4,4,4,4,5,128]{6,5,4,2,3,1,0:T(8,128)(2,1)} %bitcast.84) | data formatting | bytes 5242880 | tf_op jit(solution)/shard_map/transpose | solution.py:82
  262.7 7.0 %reshape_squeeze.6 = bf16[8,4,4,4,4,5,128]{6,5,4,3,2,1,0:T(8,128)(2,1)} reshape(bf16[1,8,16,16,640]{4,3,2,1,0:T(8,128)(2,1)} %get-tuple-element.8) | data formatting | bytes 5242880 | tf_op jit(solution)/shard_map/reshape;squeeze | solution.py:81
  269.8 3.7 %copy.32 = bf16[8,4,4,4,4,5,128]{6,4,3,5,2,1,0:T(4,128)(2,1)S(1)} copy(bf16[8,4,4,4,4,5,128]{6,5,4,2,3,1,0:T(8,128)(2,1)} %bitcast.85) | data formatting | bytes 5242880 | tf_op jit(solution)/shard_map/transpose | solution.py:82
  279.5 5.7 %fusion.55 = (f32[8,2,2,5,16]{4,3,2,1,0:T(8,128)S(1)}, f32[8,2,2,5,16,144]{5,4,3,2,1,0:T(8,128)S(1)}) fusion(pred[2,2,144]{2,1,0:T(4,128)(4,1)S(1)} %broadcast_in_dim.28, bf16[8,2,2,16,5,128]{5,3,4,2,1,0:T(8,128)(2,1)S(1)} %bitcast.94, bf16[8,2,2,144,5,128]{5,3,4,2,1,0:T(8,128)(2,1)} %copy-done), kind=kOutput, calls=%fused_computation.130 | convolution fusion | flops 95846544 | bytes 8038976 | tf_op jit(solution)/shard_map/sub | solution.py:67
  285.3 4.5 %convolution_convert_fusion.1 = bf16[8,2,2,5,128,16]{4,5,3,2,1,0:T(8,128)(2,1)S(1)} fusion(bf16[8,2,2,144,5,128]{5,3,4,2,1,0:T(8,128)(2,1)} %copy-done.4, f32[8,2,2,5,16,144]{5,4,3,2,1,0:T(8,128)S(1)} %get-tuple-element.35, f32[8,2,2,5,16]{4,3,2,1,0:T(8,128)S(1)} %get-tuple-element.34), kind=kOutput, calls=%fused_computation.31 | convolution fusion | flops 95436800 | bytes 8038400 | tf_op jit(solution)/shard_map/fabhqk,fabkhd->fabqhd/dot_general | solution.py:114
  292.1 56.2 %all-gather.12.cloned.1.call-done = bf16[512,2560]{1,0:T(8,128)(2,1)} async-done(((bf16[512,640]{1,0:T(8,128)(2,1)}), bf16[512,2560]{1,0:T(8,128)(2,1)}) %all-gather.12.cloned.1.call-update) | async-done | bytes 2621456 | tf_op jit(solution)/shard_map/all_gather | solution.py:218
  348.2 8.3 %convolution_convert_fusion = bf16[512,1280]{1,0:T(8,128)(2,1)} fusion(bf16[512,2560]{1,0:T(8,128)(2,1)} %all-gather.12.cloned.1.call-done, bf16[2560,1280]{1,0:T(8,128)(2,1)} %all-gather.14.cloned.1.call-done), kind=kOutput, calls=%fused_computation.3 | convolution fusion | flops 3356098560 | bytes 10485760 | tf_op jit(solution)/shard_map/dot_general | solution.py:219
  (97 shorter events, 41.7 us)
Async XLA Ops:
  6.5 50.6 %all-gather.6.cloned.1.call-start = ((), (), s32[]{:S(2)}) async-start(), calls=%async_computation | async-start | bytes 7372800 | tf_op jit(solution)/shard_map/all_gather | solution.py:173
  7.3 98.2 %all-gather.10.cloned.1.call-start = ((), (), s32[]{:S(2)}) async-start(), calls=%async_computation.2 | async-start | bytes 7372800 | tf_op jit(solution)/shard_map/all_gather | solution.py:172
  8.0 145.9 %all-gather.8.cloned.1.call-start = ((), (), s32[]{:S(2)}) async-start(), calls=%async_computation.1 | async-start | bytes 7372800 | tf_op jit(solution)/shard_map/all_gather | solution.py:174
  8.7 283.3 %all-gather.14.cloned.1.call-start = ((), (), s32[]{:S(2)}) async-start(), calls=%async_computation.4 | async-start | bytes 7372800 | tf_op jit(solution)/shard_map/all_gather | solution.py:175
  9.3 338.9 %all-gather.12.cloned.1.call-start = ((), (), s32[]{:S(2)}) async-start(), calls=%async_computation.3 | async-start | bytes 3276800 | tf_op jit(solution)/shard_map/all_gather | solution.py:218
  65.3 59.7 %copy-start.5 = (f32[640]{0:T(1024)S(1)}, f32[640]{0:T(1024)}, u32[]{:S(2)}) copy-start(f32[640]{0:T(1024)} %param.16) | copy-start | bytes 7684
  162.6 28.7 %copy-start.6 = (f32[640]{0:T(1024)S(1)}, f32[640]{0:T(1024)}, u32[]{:S(2)}) copy-start(f32[640]{0:T(1024)} %param.15) | copy-start | bytes 7684
  163.9 17.4 %collective-permute-start = (bf16[2,8,4,4,640]{4,3,2,1,0:T(4,128)(2,1)}, bf16[2,8,4,4,640]{4,3,2,1,0:T(4,128)(2,1)S(1)}, u32[]{:S(2)}, u32[]{:S(2)}) collective-permute-start(bf16[2,8,4,4,640]{4,3,2,1,0:T(4,128)(2,1)} %get-tuple-element.9), channel_id=1, source_target_pairs={{0,12},{4,16},{8,20},{12,24},{16,28},{1,13},{5,17},{9,21},{13,25},... | collective-permute-start | bytes 983048 | tf_op jit(solution)/shard_map/ppermute | solution.py:20
  165.2 24.1 %collective-permute-start.2 = (bf16[2,8,4,4,640]{4,3,2,1,0:T(4,128)(2,1)S(1)}, bf16[2,8,4,4,640]{4,3,2,1,0:T(4,128)(2,1)S(1)}, u32[]{:S(2)}, u32[]{:S(2)}) collective-permute-start(bf16[2,8,4,4,640]{4,3,2,1,0:T(4,128)(2,1)S(1)} %get-tuple-element.10), channel_id=1, source_target_pairs={{0,4},{4,8},{8,12},{12,16},{16,20},{20,24},{24,28},{1,5},{5,9},{9,... | collective-permute-start | bytes 983048 | tf_op jit(solution)/shard_map/ppermute | solution.py:20
  168.2 24.9 %collective-permute-start.5 = (bf16[2,8,4,4,640]{4,3,2,1,0:T(4,128)(2,1)S(1)}, bf16[2,8,4,4,640]{4,3,2,1,0:T(4,128)(2,1)S(1)}, u32[]{:S(2)}, u32[]{:S(2)}) collective-permute-start(bf16[2,8,4,4,640]{4,3,2,1,0:T(4,128)(2,1)S(1)} %get-tuple-element.11), channel_id=1, source_target_pairs={{4,0},{8,4},{12,8},{16,12},{20,16},{24,20},{28,24},{5,1},{9,5},{13... | collective-permute-start | bytes 983048 | tf_op jit(solution)/shard_map/ppermute | solution.py:20
  174.1 72.8 %collective-permute-start.1 = (bf16[2,8,4,8,640]{4,3,2,1,0:T(8,128)(2,1)}, bf16[2,8,4,8,640]{4,3,2,1,0:T(8,128)(2,1)}, u32[]{:S(2)}, u32[]{:S(2)}) collective-permute-start(bf16[2,8,4,8,640]{4,3,2,1,0:T(8,128)(2,1)} %get-tuple-element.13), channel_id=1, source_target_pairs={{0,8},{4,12},{8,16},{12,20},{16,24},{20,28},{1,9},{5,13},{9,17},{1... | collective-permute-start | bytes 1966088 | tf_op jit(solution)/shard_map/ppermute | solution.py:20
  176.0 70.8 %collective-permute-start.3 = (bf16[2,8,8,4,640]{4,3,2,1,0:T(4,128)(2,1)}, bf16[2,8,8,4,640]{4,3,2,1,0:T(4,128)(2,1)}, u32[]{:S(2)}, u32[]{:S(2)}) collective-permute-start(bf16[2,8,8,4,640]{4,3,2,1,0:T(4,128)(2,1)} %get-tuple-element.15), channel_id=1, source_target_pairs={{0,4},{4,8},{8,12},{12,16},{16,20},{20,24},{24,28},{1,5},{5,9},{9,... | collective-permute-start | bytes 1966088 | tf_op jit(solution)/shard_map/ppermute | solution.py:20
  181.3 14.4 %copy-start.1 = (bf16[2,8,4,4,640]{4,3,2,1,0:T(4,128)(2,1)}, bf16[2,8,4,4,640]{4,3,2,1,0:T(4,128)(2,1)S(1)}, u32[]{:S(2)}) copy-start(bf16[2,8,4,4,640]{4,3,2,1,0:T(4,128)(2,1)S(1)} %collective-permute-done) | copy-start | bytes 983044
  181.3 65.5 %collective-permute-start.4 = (bf16[2,8,8,4,640]{4,3,2,1,0:T(4,128)(2,1)}, bf16[2,8,8,4,640]{4,3,2,1,0:T(4,128)(2,1)}, u32[]{:S(2)}, u32[]{:S(2)}) collective-permute-start(bf16[2,8,8,4,640]{4,3,2,1,0:T(4,128)(2,1)} %get-tuple-element.16), channel_id=1, source_target_pairs={{4,0},{8,4},{12,8},{16,12},{20,16},{24,20},{28,24},{5,1},{9,5},{13... | collective-permute-start | bytes 1966088 | tf_op jit(solution)/shard_map/ppermute | solution.py:20
  189.3 7.7 %copy-start.2 = (bf16[2,8,4,4,640]{4,3,2,1,0:T(4,128)(2,1)}, bf16[2,8,4,4,640]{4,3,2,1,0:T(4,128)(2,1)S(1)}, u32[]{:S(2)}) copy-start(bf16[2,8,4,4,640]{4,3,2,1,0:T(4,128)(2,1)S(1)} %collective-permute-done.2) | copy-start | bytes 983044
  189.3 57.5 %collective-permute-start.6 = (bf16[2,8,4,8,640]{4,3,2,1,0:T(8,128)(2,1)}, bf16[2,8,4,8,640]{4,3,2,1,0:T(8,128)(2,1)}, u32[]{:S(2)}, u32[]{:S(2)}) collective-permute-start(bf16[2,8,4,8,640]{4,3,2,1,0:T(8,128)(2,1)} %get-tuple-element.14), channel_id=1, source_target_pairs={{8,0},{12,4},{16,8},{20,12},{24,16},{28,20},{9,1},{13,5},{17,9},{2... | collective-permute-start | bytes 1966088 | tf_op jit(solution)/shard_map/ppermute | solution.py:20
  193.1 4.5 %copy-start.3 = (bf16[2,8,4,4,640]{4,3,2,1,0:T(4,128)(2,1)}, bf16[2,8,4,4,640]{4,3,2,1,0:T(4,128)(2,1)S(1)}, u32[]{:S(2)}) copy-start(bf16[2,8,4,4,640]{4,3,2,1,0:T(4,128)(2,1)S(1)} %collective-permute-done.5) | copy-start | bytes 983044
  193.1 53.7 %collective-permute-start.7 = (bf16[2,8,4,4,640]{4,3,2,1,0:T(4,128)(2,1)}, bf16[2,8,4,4,640]{4,3,2,1,0:T(4,128)(2,1)}, u32[]{:S(2)}, u32[]{:S(2)}) collective-permute-start(bf16[2,8,4,4,640]{4,3,2,1,0:T(4,128)(2,1)} %get-tuple-element.12), channel_id=1, source_target_pairs={{12,0},{16,4},{20,8},{24,12},{28,16},{13,1},{17,5},{21,9},{25,13},... | collective-permute-start | bytes 983048 | tf_op jit(solution)/shard_map/ppermute | solution.py:20
  274.5 2.5 copy-start
  277.1 2.5 copy-start.4
  285.3 5.0 %copy-start.7 = (f32[64,5,8,8]{2,3,1,0:T(8,128)S(1)}, f32[64,5,8,8]{2,3,1,0:T(8,128)}, u32[]{:S(2)}) copy-start(f32[64,5,8,8]{2,3,1,0:T(8,128)} %get-tuple-element.37) | copy-start | bytes 245764
  285.3 5.0 %copy-start.8 = (f32[64,5,8]{2,1,0:T(8,128)S(1)}, f32[64,5,8]{2,1,0:T(8,128)}, u32[]{:S(2)}) copy-start(f32[64,5,8]{2,1,0:T(8,128)} %get-tuple-element.36) | copy-start | bytes 30724
Sparse Core Ops, SparseCore 0:
  9.2 47.8 all-gather.5
  59.0 46.4 all-gather.9
  107.4 46.4 all-gather.7
  155.7 73.1 all-gather.13
  292.1 56.0 all-gather.11
where the time goes:
time: 365 us; the launch traced here: 363 us
  waiting for transfers between devices  209 us (57%)
  matrix products  51.4 us (14%)
  local copies, waits for them, and re-layouts  40.9 us (11%)
  starting transfers between devices  23.4 us (6%)
  other arithmetic  15.2 us (4%)
  between operations  13.7 us (4%)
  blocking collectives  9.83 us (3%)
    all_gather x1, waiting for transfers between devices, per_device(): lax.all_gather(mixed.reshape(-1, group_width), 'head', axis=1, tiled=True)  56.2 us
    ppermute x8, waiting for transfers between devices, from_behind(): lax.ppermute(value, axis, [(source, source + steps) for source in range(i...  49.2 us
    all_gather x1, waiting for transfers between devices, per_device(): lax.all_gather(query_weight, 'hw', axis=0, tiled=True)  40.2 us
    all_gather x1, waiting for transfers between devices, per_device(): lax.all_gather(key_weight, 'hw', axis=0, tiled=True)  33 us
    all_gather x1, waiting for transfers between devices, per_device(): lax.all_gather(value_weight, 'hw', axis=0, tiled=True)  27.5 us
    ppermute x8, starting transfers between devices, from_behind(): lax.ppermute(value, axis, [(source, source + steps) for source in range(i...  23.2 us
    another operation x2, local copies, waits for them, and re-layouts, tiles(): array.reshape(frames, across + extra, WT, along + extra, WT, heads_here,...  11.2 us
    psum x1, blocking collectives, per_device(): lax.psum((jnp.sum(query_lin * query_lin, axis=1), jnp.sum(key_lin * key_l...  9.83 us
  transfers between devices with their start and end apart: 13, of which 6 were waited for; matrix products, arithmetic and copies ran while one was open for 26% of the time, Pallas kernels for 0%

commit v1 on v0

--- a/solution.py
+++ b/solution.py
@@ -1,8 +1,11 @@
+import functools
 import math
 
 import jax
 import jax.numpy as jnp
 from jax import lax
+from jax.experimental import pallas as pl
+from jax.experimental.pallas import tpu as pltpu
 from jax.sharding import PartitionSpec as P
 
 HEADS = 20
@@ -143,6 +146,222 @@
         (columns - edge, columns) if right < 0 else (0, edge) if right > 0 else (0, columns)
     )
     return stack[:, :, row_start:row_stop, column_start:column_stop]
+
+
+CUBE = 8
+
+
+class Cube:
+    def __init__(self, stride):
+        me = lax.axis_index("hw")
+        within = lax.rem(me, stride) if stride > 1 else 0
+        place = lax.div(me, stride) if stride > 1 else me
+        core = lax.rem(place, 2)
+        x = lax.rem(lax.div(place, 2), 2)
+        y = lax.div(place, 4)
+        self.place = place
+        self.other = [place + 1 - 2 * core, place + 2 - 4 * x, place + 4 - 8 * y]
+        self.diagonal = place + 2 - 4 * x + 4 - 8 * y
+        self.devices = [{"hw": other * stride + within} for other in self.other]
+        self.chip = lax.div(place, 2)
+        self.chips = [
+            self.chip,
+            self.chip + 1 - 2 * x,
+            self.chip + 2 - 4 * y,
+            self.chip + 3 - 2 * x - 4 * y,
+        ]
+
+    def barrier(self):
+        semaphore = pltpu.get_barrier_semaphore()
+        for device in self.devices:
+            pl.semaphore_signal(semaphore, inc=1, device_id=device, device_id_type=pl.DeviceIdType.MESH)
+        pl.semaphore_wait(semaphore, len(self.devices))
+
+
+class Exchange:
+    def __init__(self, cube, held, send, receive, rows):
+        core_place, x_place, y_place = cube.other
+        half = rows // 2
+
+        def part(place, low, size):
+            start = pl.multiple_of(lax.rem(place, 2) * rows + low, 16)
+            return held.at[lax.div(place, 2), pl.ds(start, size)]
+
+        def copy(at, place, low, size, partner):
+            ref = part(place, low, size)
+            return pltpu.make_async_remote_copy(
+                src_ref=ref,
+                dst_ref=ref,
+                send_sem=send.at[at],
+                recv_sem=receive.at[at],
+                device_id=cube.devices[partner],
+                device_id_type=pl.DeviceIdType.MESH,
+            )
+
+        self.own = part(cube.place, 0, rows)
+        self.copies = [
+            copy(0, cube.place, 0, rows, 1),
+            copy(1, cube.place, 0, rows, 2),
+            copy(2, cube.place, 0, rows, 0),
+            copy(3, x_place, 0, rows, 0),
+            copy(4, y_place, 0, rows, 0),
+            copy(5, x_place, 0, half, 2),
+            copy(6, y_place, half, half, 1),
+            copy(7, cube.diagonal, 0, half, 0),
+            copy(8, cube.diagonal, half, half, 0),
+        ]
+
+    def start(self, *which):
+        for at in which:
+            self.copies[at].start()
+
+    def arrived(self, *which):
+        for at in which:
+            self.copies[at].wait_recv()
+
+    def sent(self):
+        for one in self.copies:
+            one.wait_send()
+
+
+def project_kernel(
+    stride, tokens_hbm, query_hbm, key_hbm, value_hbm, output_hbm,
+    query_ref, key_ref, value_ref, output_all,
+    tokens, held, value_sum, local, send, receive,
+):
+    cube = Cube(stride)
+    rows = query_hbm.shape[0]
+    depth = 2 * rows
+    weights = [
+        Exchange(cube, held.at[at], send.at[at], receive.at[at], rows) for at in range(3)
+    ] + [Exchange(cube, output_all, send.at[3], receive.at[3], output_hbm.shape[0])]
+    loads = [
+        pltpu.make_async_copy(source, weight.own, local.at[at])
+        for at, (source, weight) in enumerate(
+            zip((query_hbm, key_hbm, value_hbm, output_hbm), weights)
+        )
+    ]
+    fetch = pltpu.make_async_copy(tokens_hbm, tokens, local.at[4])
+    for load in loads:
+        load.start()
+    fetch.start()
+    cube.barrier()
+    query, key, value, output = weights
+    loads[0].wait()
+    query.start(2, 0, 1)
+    loads[1].wait()
+    key.start(2, 0, 1)
+    sums = [query_ref, key_ref, value_sum]
+    block = tokens.shape[0] // 2
+
+    def multiply(at, lane):
+        chip = cube.chips[lane]
+
+        @pl.loop(0, 2)
+        def _(step):
+            here = pl.ds(pl.multiple_of(step * block, block), block)
+            product = jnp.dot(
+                tokens[here, pl.ds(pl.multiple_of(chip * depth, 128), depth)],
+                held[at, chip],
+                preferred_element_type=jnp.float32,
+            )
+            if lane == 0:
+                sums[at][here, :] = product
+            else:
+                sums[at][here, :] += product
+
+    def near(weight):
+        weight.arrived(0)
+        weight.start(5, 3)
+        weight.arrived(1)
+        weight.start(6, 4)
+
+    def far(weight):
+        weight.arrived(5)
+        weight.start(7)
+        weight.arrived(6)
+        weight.start(8)
+
+    def near_multiply(at):
+        weights[at].arrived(3)
+        multiply(at, 1)
+        weights[at].arrived(4)
+        multiply(at, 2)
+
+    def far_multiply(at):
+        weights[at].arrived(7, 8)
+        multiply(at, 3)
+
+    loads[2].wait()
+    loads[3].wait()
+    fetch.wait()
+    query.arrived(2)
+    multiply(0, 0)
+    key.arrived(2)
+    multiply(1, 0)
+    near(query)
+    near_multiply(0)
+    near(key)
+    value.start(2, 0, 1)
+    output.start(2, 0, 1)
+    near_multiply(1)
+    value.arrived(2)
+    multiply(2, 0)
+    far(query)
+    far_multiply(0)
+    far(key)
+    far_multiply(1)
+    near(value)
+    near_multiply(2)
+    near(output)
+    far(value)
+    far_multiply(2)
+    value_ref[...] = value_sum[...].astype(value_ref.dtype)
+    output.arrived(2, 3, 4)
+    far(output)
+    output.arrived(7, 8)
+    for weight in weights:
+        weight.sent()
+
+
+def project(tokens, query_weight, key_weight, value_weight, output_weight, stride):
+    count = tokens.shape[0]
+    rows, width = query_weight.shape
+    output_rows, output_width = output_weight.shape
+    anywhere = pl.BlockSpec(memory_space=pl.ANY)
+    vmem = pl.BlockSpec(memory_space=pltpu.VMEM)
+    query, key, value, output = pl.pallas_call(
+        functools.partial(project_kernel, stride),
+        out_shape=(
+            jax.ShapeDtypeStruct((count, width), jnp.float32),
+            jax.ShapeDtypeStruct((count, width), jnp.float32),
+            jax.ShapeDtypeStruct((count, width), jnp.bfloat16),
+            jax.ShapeDtypeStruct((CUBE // 2, 2 * output_rows, output_width), jnp.bfloat16),
+        ),
+        in_specs=[anywhere] * 5,
+        out_specs=(vmem, vmem, vmem, anywhere),
+        scratch_shapes=[
+            pltpu.VMEM(tokens.shape, tokens.dtype),
+            pltpu.VMEM((3, CUBE // 2, 2 * rows, width), query_weight.dtype),
+            pltpu.VMEM((count, width), jnp.float32),
+            pltpu.SemaphoreType.DMA((5,)),
+            pltpu.SemaphoreType.DMA((4, 9)),
+            pltpu.SemaphoreType.DMA((4, 9)),
+        ],
+        compiler_params=pltpu.CompilerParams(
+            collective_id=0, has_side_effects=True, vmem_limit_bytes=60 * 1024 * 1024
+        ),
+        name="project",
+    )(tokens, query_weight, key_weight, value_weight, output_weight)
+    return query, key, value, output.reshape(-1, output_width)
+
+
+def pregather(weight, stride):
+    if stride == 1:
+        return weight
+    count = lax.axis_size("hw")
+    groups = [list(range(first, first + stride)) for first in range(0, count, stride)]
+    return lax.all_gather(weight, "hw", axis=0, tiled=True, axis_index_groups=groups)
 
 
 def per_device(
@@ -168,16 +387,12 @@
     grid_row = place // grid_columns
     grid_column = place % grid_columns
     tiles_side = side // WT
-    query_all, key_all, value_all, output_all = (
-        lax.all_gather(query_weight, "hw", axis=0, tiled=True),
-        lax.all_gather(key_weight, "hw", axis=0, tiled=True),
-        lax.all_gather(value_weight, "hw", axis=0, tiled=True),
-        lax.all_gather(output_weight, "hw", axis=0, tiled=True),
-    )
-    query_lin = jnp.dot(tokens, query_all, preferred_element_type=jnp.float32)
-    key_lin = jnp.dot(tokens, key_all, preferred_element_type=jnp.float32)
-    value_lin = jnp.dot(tokens, value_all, preferred_element_type=jnp.float32)
-    values = value_lin.astype(jnp.bfloat16)
+    stride = lax.axis_size("hw") // CUBE
+    query_lin, key_lin, values, output_all = project(
+        tokens,
+        *(pregather(w, stride) for w in (query_weight, key_weight, value_weight, output_weight)),
+        stride,
+    )
     query_squares, key_squares = lax.psum(
         (jnp.sum(query_lin * query_lin, axis=1), jnp.sum(key_lin * key_lin, axis=1)), "head"
     )

time: 365 us -> 331 us (0.907)
  waiting for transfers between devices: 209 us -> 80.5 us
  Pallas kernels: 0 us -> 114 us
  matrix products: 51.4 us -> 26 us
    pallas_call x0 -> x1, Pallas kernels: none -> 114 us  [project(): pl.pallas_call(functools.partial(project_kernel, stride), out_shape=(jax....]
    all_gather x4 -> x0, waiting for transfers between devices: 101 us -> none  [the longest x1 40.2 us: per_device(): lax.all_gather(query_weight, 'hw', axis=0, tiled=True)]
    dot_general x3 -> x0, matrix products: 26.6 us -> none  [the longest x1 9.7 us: per_device(): query_lin = jnp.dot(tokens, query_all, preferred_element_type=jnp.float32)]
    ppermute x8, waiting for transfers between devices: 49.2 us -> 27 us  [from_behind(): lax.ppermute(value, axis, [(source, source + steps) for source in range(i...]
    unnamed x35 -> x37, local copies, waits for them, and re-layouts: 6.73 us -> 7.59 us
  transfers between devices with their start and end apart: 13 -> 9, of which waited for: 6 -> 3; matrix products, arithmetic and copies ran while one was open for 26% -> 3% of each run, Pallas kernels for 0% -> 0%
where the time goes in v1:
time: 331 us; the launch traced here: 329 us
  Pallas kernels  114 us (34%)
  waiting for transfers between devices  80.5 us (24%)
  local copies, waits for them, and re-layouts  43.1 us (13%)
  matrix products  26 us (8%)
  starting transfers between devices  23.6 us (7%)
  other arithmetic  17.9 us (5%)
  between operations  14 us (4%)
  blocking collectives  10.1 us (3%)
    pallas_call x1, Pallas kernels, project(): pl.pallas_call(functools.partial(project_kernel, stride), out_shape=(jax....  114 us
    all_gather x1, waiting for transfers between devices, per_device(): lax.all_gather(mixed.reshape(-1, group_width), 'head', axis=1, tiled=True)  53.4 us
    ppermute x8, waiting for transfers between devices, from_behind(): lax.ppermute(value, axis, [(source, source + steps) for source in range(i...  27 us
    ppermute x8, starting transfers between devices, from_behind(): lax.ppermute(value, axis, [(source, source + steps) for source in range(i...  23.6 us
    another operation x2, local copies, waits for them, and re-layouts, tiles(): array.reshape(frames, across + extra, WT, along + extra, WT, heads_here,...  11.2 us
    sub x2, matrix products, soft_weights(): raised = jnp.exp(scores - top)  10.2 us
    psum x1, blocking collectives, per_device(): lax.psum((jnp.sum(query_lin * query_lin, axis=1), jnp.sum(key_lin * key_l...  10.1 us
    dot_general x1, matrix products, per_device(): result = jnp.dot(gathered, output_all, preferred_element_type=jnp.float32)  8.26 us
  transfers between devices with their start and end apart: 9, of which 3 were waited for; matrix products, arithmetic and copies ran while one was open for 3% of the time, Pallas kernels for 0%

profile of v1, /device:TPU:5, one launch (start us, length us, event | category | flops | bytes accessed | tf_op | source)
XLA Modules:
  0.0 328.8 jit_solution(10985789605090176415)
XLA Ops:
  10.1 2.2 broadcast_in_dim.25
  12.4 2.8 copy.29
  18.1 2.8 copy.31
  20.9 113.5 %project.1 = (f32[512,640]{1,0:T(8,128)}, f32[512,640]{1,0:T(8,128)}, bf16[512,640]{1,0:T(8,128)(2,1)}, bf16[4,640,1280]{2,1,0:T(8,128)(2,1)}) custom-call(bf16[512,5120]{1,0:T(8,128)(2,1)} %bitcast.86, bf16[640,640]{1,0:T(8,128)(2,1)} %query_hbm.1, bf16[640,640]{1,0:T(8,128)(2,1)} %key_hbm.1, bf16[640,640]{1,0:T(8,128)(2,1)} %value_hbm.1, ...), custom_call_target="tpu_custom_call" | custom-call | tf_op jit(solution)/shard_map/project/pallas_call | solution.py:333
  137.5 10.1 %all-reduce = (f32[512]{0:T(512)S(1)}, f32[512]{0:T(512)S(1)}) all-reduce(f32[512]{0:T(512)S(1)} %multiply_reduce_fusion.1, f32[512]{0:T(512)S(1)} %multiply_reduce_fusion), channel_id=1, replica_groups=mesh['hw'=8,'head'=4] {'head'}, use_global_device_ids=true, to_apply=%region_1.2 | all-reduce | flops 1024 | bytes 8192 | tf_op jit(solution)/shard_map/psum | solution.py:396
  152.6 4.8 %collective-permute-start.3 = (bf16[2,8,8,4,640]{4,3,2,1,0:T(4,128)(2,1)}, bf16[2,8,8,4,640]{4,3,2,1,0:T(4,128)(2,1)S(1)}, u32[]{:S(2)}, u32[]{:S(2)}) collective-permute-start(bf16[2,8,8,4,640]{4,3,2,1,0:T(4,128)(2,1)} %get-tuple-element.23), channel_id=1, source_target_pairs={{0,4},{4,8},{8,12},{12,16},{16,20},{20,24},{24,28},{1,5},{5,9},{9,... | collective-permute-start | bytes 1966088 | tf_op jit(solution)/shard_map/ppermute | solution.py:23
  162.0 3.6 %collective-permute-start.2 = (bf16[2,8,4,4,640]{4,3,2,1,0:T(4,128)(2,1)}, bf16[2,8,4,4,640]{4,3,2,1,0:T(4,128)(2,1)}, u32[]{:S(2)}, u32[]{:S(2)}) collective-permute-start(bf16[2,8,4,4,640]{4,3,2,1,0:T(4,128)(2,1)} %get-tuple-element.18), channel_id=1, source_target_pairs={{0,4},{4,8},{8,12},{12,16},{16,20},{20,24},{24,28},{1,5},{5,9},{9,... | collective-permute-start | bytes 983048 | tf_op jit(solution)/shard_map/ppermute | solution.py:23
  165.7 2.6 collective-permute-start.5
  170.8 10.2 %collective-permute-done = bf16[2,8,4,4,640]{4,3,2,1,0:T(4,128)(2,1)S(1)} collective-permute-done((bf16[2,8,4,4,640]{4,3,2,1,0:T(4,128)(2,1)}, bf16[2,8,4,4,640]{4,3,2,1,0:T(4,128)(2,1)S(1)}, u32[]{:S(2)}, u32[]{:S(2)}) %collective-permute-start) | collective-permute-done | bytes 327712 | tf_op jit(solution)/shard_map/ppermute | solution.py:23
  183.0 4.2 %collective-permute-start.6 = (bf16[2,8,4,8,640]{4,3,2,1,0:T(8,128)(2,1)}, bf16[2,8,4,8,640]{4,3,2,1,0:T(8,128)(2,1)}, u32[]{:S(2)}, u32[]{:S(2)}) collective-permute-start(bf16[2,8,4,8,640]{4,3,2,1,0:T(8,128)(2,1)} %get-tuple-element.22), channel_id=1, source_target_pairs={{8,0},{12,4},{16,8},{20,12},{24,16},{28,20},{9,1},{13,5},{17,9},{2... | collective-permute-start | bytes 1966088 | tf_op jit(solution)/shard_map/ppermute | solution.py:23
  187.3 3.2 collective-permute-start.7
  193.1 4.6 %fusion.56 = (f32[64,5,8]{2,1,0:T(8,128)}, f32[64,5,8,8]{2,3,1,0:T(8,128)}) fusion(bf16[8,64,5,128]{3,1,2,0:T(8,128)(2,1)} %bitcast.92, bf16[8,64,5,128]{3,1,2,0:T(8,128)(2,1)} %bitcast.93), kind=kOutput, calls=%fused_computation.130 | convolution fusion | flops 5304327 | bytes 1402880 | tf_op jit(solution)/shard_map/sub | solution.py:70
  197.6 16.7 %collective-permute-done.7 = bf16[2,8,4,4,640]{4,3,2,1,0:T(4,128)(2,1)} collective-permute-done((bf16[2,8,4,4,640]{4,3,2,1,0:T(4,128)(2,1)}, bf16[2,8,4,4,640]{4,3,2,1,0:T(4,128)(2,1)}, u32[]{:S(2)}, u32[]{:S(2)}) %collective-permute-start.7) | collective-permute-done | bytes 327712 | tf_op jit(solution)/shard_map/ppermute | solution.py:23
  214.4 5.7 %maximum_maximum_fusion = bf16[2,8,16,16,640]{4,3,2,1,0:T(8,128)(2,1)S(1)} fusion(bf16[2,8,4,4,640]{4,3,2,1,0:T(4,128)(2,1)} %collective-permute-done.7, bf16[2,8,4,8,640]{4,3,2,1,0:T(8,128)(2,1)} %collective-permute-done.6, bf16[2,8,4,4,640]{4,3,2,1,0:T(4,128)(2,1)} %collective-permute-done.5, bf16[2,8,8,4,640]{4,3,2,1,0:T(4,128)(2,1)} %collective-permute-done.4, ...), kind=kLoop, calls=%fused_computation.2 | loop fusion | flops 52428800 | bytes 10485760 | tf_op jit(solution)/shard_map/concatenate | solution.py:420
  222.2 7.0 %reshape_squeeze.7 = bf16[8,4,4,4,4,5,128]{6,5,4,3,2,1,0:T(8,128)(2,1)} reshape(bf16[1,8,16,16,640]{4,3,2,1,0:T(8,128)(2,1)} %get-tuple-element.15) | data formatting | bytes 5242880 | tf_op jit(solution)/shard_map/reshape;squeeze | solution.py:84
  229.2 3.7 %copy.34 = bf16[8,4,4,4,4,5,128]{6,4,3,5,2,1,0:T(4,128)(2,1)S(1)} copy(bf16[8,4,4,4,4,5,128]{6,5,4,2,3,1,0:T(8,128)(2,1)} %bitcast.79) | data formatting | bytes 5242880 | tf_op jit(solution)/shard_map/transpose | solution.py:85
  233.9 2.5 copy-done.1
  236.4 4.2 %reshape_squeeze.6 = bf16[8,4,4,4,4,5,128]{6,5,4,3,2,1,0:T(8,128)(2,1)} reshape(bf16[1,8,16,16,640]{4,3,2,1,0:T(8,128)(2,1)S(1)} %get-tuple-element.16) | data formatting | bytes 5242880 | tf_op jit(solution)/shard_map/reshape;squeeze | solution.py:84
  240.6 3.7 %copy.32 = bf16[8,4,4,4,4,5,128]{6,4,3,5,2,1,0:T(4,128)(2,1)S(1)} copy(bf16[8,4,4,4,4,5,128]{6,5,4,2,3,1,0:T(8,128)(2,1)} %bitcast.80) | data formatting | bytes 5242880 | tf_op jit(solution)/shard_map/transpose | solution.py:85
  245.3 2.5 copy-done.5
  247.8 5.7 %fusion.55 = (f32[8,2,2,5,16]{4,3,2,1,0:T(8,128)S(1)}, f32[8,2,2,5,16,144]{5,4,3,2,1,0:T(8,128)S(1)}) fusion(pred[2,2,144]{2,1,0:T(4,128)(4,1)S(1)} %broadcast_in_dim.28, bf16[8,2,2,16,5,128]{5,3,4,2,1,0:T(8,128)(2,1)S(1)} %bitcast.90, bf16[8,2,2,144,5,128]{5,3,4,2,1,0:T(8,128)(2,1)} %copy-done.1), kind=kOutput, calls=%fused_computation.129 | convolution fusion | flops 95846544 | bytes 8038976 | tf_op jit(solution)/shard_map/sub | solution.py:70
  253.5 4.5 %convolution_convert_fusion.1 = bf16[8,2,2,5,128,16]{4,5,3,2,1,0:T(8,128)(2,1)S(1)} fusion(bf16[8,2,2,144,5,128]{5,3,4,2,1,0:T(8,128)(2,1)} %copy-done.5, f32[8,2,2,5,16,144]{5,4,3,2,1,0:T(8,128)S(1)} %get-tuple-element.39, f32[8,2,2,5,16]{4,3,2,1,0:T(8,128)S(1)} %get-tuple-element.38), kind=kOutput, calls=%fused_computation.31 | convolution fusion | flops 95436800 | bytes 8038400 | tf_op jit(solution)/shard_map/fabhqk,fabkhd->fabqhd/dot_general | solution.py:117
  260.2 53.4 %all-gather.2.cloned.1.call-done = bf16[512,2560]{1,0:T(8,128)(2,1)} async-done(((bf16[512,640]{1,0:T(8,128)(2,1)}), bf16[512,2560]{1,0:T(8,128)(2,1)}) %all-gather.2.cloned.1.call-update) | async-done | bytes 2621456 | tf_op jit(solution)/shard_map/all_gather | solution.py:433
  313.7 8.3 %convolution_convert_fusion = bf16[512,1280]{1,0:T(8,128)(2,1)} fusion(bf16[512,2560]{1,0:T(8,128)(2,1)} %all-gather.2.cloned.1.call-done, bf16[2560,1280]{1,0:T(8,128)(2,1)} %bitcast.96), kind=kOutput, calls=%fused_computation.3 | convolution fusion | flops 3356098560 | bytes 10485760 | tf_op jit(solution)/shard_map/dot_general | solution.py:434
  (87 shorter events, 32.2 us)
Async XLA Ops:
  6.5 307.1 %all-gather.2.cloned.1.call-start = ((), (), s32[]{:S(2)}) async-start(), calls=%async_computation | async-start | bytes 3276800 | tf_op jit(solution)/shard_map/all_gather | solution.py:433
  134.4 13.2 %copy-start.2 = (f32[512,640]{1,0:T(8,128)S(1)}, f32[512,640]{1,0:T(8,128)}, u32[]{:S(2)}) copy-start(f32[512,640]{1,0:T(8,128)} %get-tuple-element.11) | copy-start | bytes 3932164
  134.4 13.2 %copy-start.6 = (f32[640]{0:T(1024)S(1)}, f32[640]{0:T(1024)}, u32[]{:S(2)}) copy-start(f32[640]{0:T(1024)} %param.15) | copy-start | bytes 7684
  134.5 13.2 %copy-start.7 = (f32[640]{0:T(1024)S(1)}, f32[640]{0:T(1024)}, u32[]{:S(2)}) copy-start(f32[640]{0:T(1024)} %param.16) | copy-start | bytes 7684
  147.7 2.9 copy-start
  152.6 61.8 %collective-permute-start.3 = (bf16[2,8,8,4,640]{4,3,2,1,0:T(4,128)(2,1)}, bf16[2,8,8,4,640]{4,3,2,1,0:T(4,128)(2,1)S(1)}, u32[]{:S(2)}, u32[]{:S(2)}) collective-permute-start(bf16[2,8,8,4,640]{4,3,2,1,0:T(4,128)(2,1)} %get-tuple-element.23), channel_id=1, source_target_pairs={{0,4},{4,8},{8,12},{12,16},{16,20},{20,24},{24,28},{1,5},{5,9},{9,... | collective-permute-start | bytes 1966088 | tf_op jit(solution)/shard_map/ppermute | solution.py:23
  157.4 57.0 %collective-permute-start.4 = (bf16[2,8,8,4,640]{4,3,2,1,0:T(4,128)(2,1)}, bf16[2,8,8,4,640]{4,3,2,1,0:T(4,128)(2,1)}, u32[]{:S(2)}, u32[]{:S(2)}) collective-permute-start(bf16[2,8,8,4,640]{4,3,2,1,0:T(4,128)(2,1)} %get-tuple-element.24), channel_id=1, source_target_pairs={{4,0},{8,4},{12,8},{16,12},{20,16},{24,20},{28,24},{5,1},{9,5},{13... | collective-permute-start | bytes 1966088 | tf_op jit(solution)/shard_map/ppermute | solution.py:23
  160.8 20.3 %collective-permute-start = (bf16[2,8,4,4,640]{4,3,2,1,0:T(4,128)(2,1)}, bf16[2,8,4,4,640]{4,3,2,1,0:T(4,128)(2,1)S(1)}, u32[]{:S(2)}, u32[]{:S(2)}) collective-permute-start(bf16[2,8,4,4,640]{4,3,2,1,0:T(4,128)(2,1)} %get-tuple-element.17), channel_id=1, source_target_pairs={{0,12},{4,16},{8,20},{12,24},{16,28},{1,13},{5,17},{9,21},{13,25},... | collective-permute-start | bytes 983048 | tf_op jit(solution)/shard_map/ppermute | solution.py:23
  162.0 20.9 %collective-permute-start.2 = (bf16[2,8,4,4,640]{4,3,2,1,0:T(4,128)(2,1)}, bf16[2,8,4,4,640]{4,3,2,1,0:T(4,128)(2,1)}, u32[]{:S(2)}, u32[]{:S(2)}) collective-permute-start(bf16[2,8,4,4,640]{4,3,2,1,0:T(4,128)(2,1)} %get-tuple-element.18), channel_id=1, source_target_pairs={{0,4},{4,8},{8,12},{12,16},{16,20},{20,24},{24,28},{1,5},{5,9},{9,... | collective-permute-start | bytes 983048 | tf_op jit(solution)/shard_map/ppermute | solution.py:23
  165.7 21.6 %collective-permute-start.5 = (bf16[2,8,4,4,640]{4,3,2,1,0:T(4,128)(2,1)}, bf16[2,8,4,4,640]{4,3,2,1,0:T(4,128)(2,1)}, u32[]{:S(2)}, u32[]{:S(2)}) collective-permute-start(bf16[2,8,4,4,640]{4,3,2,1,0:T(4,128)(2,1)} %get-tuple-element.19), channel_id=1, source_target_pairs={{4,0},{8,4},{12,8},{16,12},{20,16},{24,20},{28,24},{5,1},{9,5},{13... | collective-permute-start | bytes 983048 | tf_op jit(solution)/shard_map/ppermute | solution.py:23
  181.0 11.5 %copy-start.3 = (bf16[2,8,4,4,640]{4,3,2,1,0:T(4,128)(2,1)}, bf16[2,8,4,4,640]{4,3,2,1,0:T(4,128)(2,1)S(1)}, u32[]{:S(2)}) copy-start(bf16[2,8,4,4,640]{4,3,2,1,0:T(4,128)(2,1)S(1)} %collective-permute-done) | copy-start | bytes 983044
  181.0 33.4 %collective-permute-start.1 = (bf16[2,8,4,8,640]{4,3,2,1,0:T(8,128)(2,1)}, bf16[2,8,4,8,640]{4,3,2,1,0:T(8,128)(2,1)}, u32[]{:S(2)}, u32[]{:S(2)}) collective-permute-start(bf16[2,8,4,8,640]{4,3,2,1,0:T(8,128)(2,1)} %get-tuple-element.21), channel_id=1, source_target_pairs={{0,8},{4,12},{8,16},{12,20},{16,24},{20,28},{1,9},{5,13},{9,17},{1... | collective-permute-start | bytes 1966088 | tf_op jit(solution)/shard_map/ppermute | solution.py:23
  183.0 31.4 %collective-permute-start.6 = (bf16[2,8,4,8,640]{4,3,2,1,0:T(8,128)(2,1)}, bf16[2,8,4,8,640]{4,3,2,1,0:T(8,128)(2,1)}, u32[]{:S(2)}, u32[]{:S(2)}) collective-permute-start(bf16[2,8,4,8,640]{4,3,2,1,0:T(8,128)(2,1)} %get-tuple-element.22), channel_id=1, source_target_pairs={{8,0},{12,4},{16,8},{20,12},{24,16},{28,20},{9,1},{13,5},{17,9},{2... | collective-permute-start | bytes 1966088 | tf_op jit(solution)/shard_map/ppermute | solution.py:23
  187.3 27.1 %collective-permute-start.7 = (bf16[2,8,4,4,640]{4,3,2,1,0:T(4,128)(2,1)}, bf16[2,8,4,4,640]{4,3,2,1,0:T(4,128)(2,1)}, u32[]{:S(2)}, u32[]{:S(2)}) collective-permute-start(bf16[2,8,4,4,640]{4,3,2,1,0:T(4,128)(2,1)} %get-tuple-element.20), channel_id=1, source_target_pairs={{12,0},{16,4},{20,8},{24,12},{28,16},{13,1},{17,5},{21,9},{25,13},... | collective-permute-start | bytes 983048 | tf_op jit(solution)/shard_map/ppermute | solution.py:23
  192.8 21.6 %copy-start.4 = (bf16[2,8,4,4,640]{4,3,2,1,0:T(4,128)(2,1)S(1)}, bf16[2,8,4,4,640]{4,3,2,1,0:T(4,128)(2,1)}, u32[]{:S(2)}) copy-start(bf16[2,8,4,4,640]{4,3,2,1,0:T(4,128)(2,1)} %copy-done.3) | copy-start | bytes 983044
  233.9 2.5 copy-start.1
  245.3 2.5 copy-start.5
  253.5 5.0 %copy-start.8 = (f32[64,5,8,8]{2,3,1,0:T(8,128)S(1)}, f32[64,5,8,8]{2,3,1,0:T(8,128)}, u32[]{:S(2)}) copy-start(f32[64,5,8,8]{2,3,1,0:T(8,128)} %get-tuple-element.41) | copy-start | bytes 245764
  253.5 5.0 %copy-start.9 = (f32[64,5,8]{2,1,0:T(8,128)S(1)}, f32[64,5,8]{2,1,0:T(8,128)}, u32[]{:S(2)}) copy-start(f32[64,5,8]{2,1,0:T(8,128)} %get-tuple-element.40) | copy-start | bytes 30724
Sparse Core Ops, SparseCore 0:
  260.4 53.2 all-gather.1

commit v2 on v1

--- a/solution.py
+++ b/solution.py
@@ -63,79 +63,6 @@
     ).reshape(shaped.shape)
     rotated = shaped * cosine + turned * sine
     return rotated.astype(jnp.bfloat16).reshape(frames, rows, columns, heads_here * head_dim)
-
-
-def soft_weights(scores):
-    top = jnp.max(scores, axis=-1, keepdims=True)
-    raised = jnp.exp(scores - top)
-    return (raised / jnp.sum(raised, axis=-1, keepdims=True)).astype(jnp.bfloat16)
-
-
-def window_attend(
-    queries, keys, values, first_row, first_column, total_rows, total_columns, heads_here, head_dim
-):
-    frames, rows, columns, width = queries.shape
-    across = rows // WT
-    along = columns // WT
-    area = WT * WT
-    scale = 1.0 / math.sqrt(head_dim)
-
-    def tiles(array, extra):
-        shaped = array.reshape(frames, across + extra, WT, along + extra, WT, heads_here, head_dim)
-        return shaped.transpose(0, 1, 3, 2, 4, 5, 6).reshape(
-            frames, across + extra, along + extra, area, heads_here, head_dim
-        )
-
-    query_tiles = tiles(queries, 0)
-    key_tiles = tiles(keys, 2)
-    value_tiles = tiles(values, 2)
-    offsets = [(down, right) for down in range(3) for right in range(3)]
-    key_window = jnp.concatenate(
-        [key_tiles[:, down : down + across, right : right + along] for down, right in offsets],
-        axis=3,
-    )
-    value_window = jnp.concatenate(
-        [value_tiles[:, down : down + across, right : right + along] for down, right in offsets],
-        axis=3,
-    )
-    tile_rows = first_row + jnp.arange(across)
-    tile_columns = first_column + jnp.arange(along)
-    inside = []
-    for down, right in offsets:
-        row_ok = (tile_rows + down - 1 >= 0) & (tile_rows + down - 1 < total_rows)
-        column_ok = (tile_columns + right - 1 >= 0) & (tile_columns + right - 1 < total_columns)
-        inside.append(row_ok[:, None] & column_ok[None, :])
-    allowed = jnp.repeat(jnp.stack(inside, axis=-1), area, axis=-1)
-    scores = (
-        jnp.einsum(
-            "fabqhd,fabkhd->fabhqk", query_tiles, key_window, preferred_element_type=jnp.float32
-        )
-        * scale
-    )
-    scores = jnp.where(allowed[None, :, :, None, None, :], scores, -jnp.inf)
-    weights = soft_weights(scores)
-    mixed = jnp.einsum(
-        "fabhqk,fabkhd->fabqhd", weights, value_window, preferred_element_type=jnp.float32
-    ).astype(jnp.bfloat16)
-    mixed = mixed.reshape(frames, across, along, WT, WT, heads_here, head_dim)
-    return mixed.transpose(0, 1, 3, 2, 4, 5, 6).reshape(frames, rows, columns, width)
-
-
-def frame_attend(queries, keys, values, heads_here, head_dim):
-    frames = queries.shape[0]
-    scale = 1.0 / math.sqrt(head_dim)
-    query_rows = queries.reshape(frames, -1, heads_here, head_dim)
-    key_rows = keys.reshape(frames, -1, heads_here, head_dim)
-    value_rows = values.reshape(frames, -1, heads_here, head_dim)
-    scores = (
-        jnp.einsum("fphd,gphd->phfg", query_rows, key_rows, preferred_element_type=jnp.float32)
-        * scale
-    )
-    weights = soft_weights(scores)
-    mixed = jnp.einsum(
-        "phfg,gphd->fphd", weights, value_rows, preferred_element_type=jnp.float32
-    ).astype(jnp.bfloat16)
-    return mixed.reshape(queries.shape)
 
 
 def region(stack, down, right, edge):
@@ -171,11 +98,16 @@
             self.chip + 3 - 2 * x - 4 * y,
         ]
 
-    def barrier(self):
+    def barrier(self, line=None):
         semaphore = pltpu.get_barrier_semaphore()
+        if line is not None:
+            line.greet(semaphore)
         for device in self.devices:
             pl.semaphore_signal(semaphore, inc=1, device_id=device, device_id_type=pl.DeviceIdType.MESH)
-        pl.semaphore_wait(semaphore, len(self.devices))
+        if line is None:
+            pl.semaphore_wait(semaphore, len(self.devices))
+        else:
+            line.meet(semaphore, len(self.devices))
 
 
 class Exchange:
@@ -219,14 +151,26 @@
         for at in which:
             self.copies[at].wait_recv()
 
+    def near(self):
+        self.arrived(0)
+        self.start(5, 3)
+        self.arrived(1)
+        self.start(6, 4)
+
+    def far(self):
+        self.arrived(5)
+        self.start(7)
+        self.arrived(6)
+        self.start(8)
+
     def sent(self):
         for one in self.copies:
             one.wait_send()
 
 
 def project_kernel(
-    stride, tokens_hbm, query_hbm, key_hbm, value_hbm, output_hbm,
-    query_ref, key_ref, value_ref, output_all,
+    stride, tokens_hbm, query_hbm, key_hbm, value_hbm,
+    query_ref, key_ref, value_ref,
     tokens, held, value_sum, local, send, receive,
 ):
     cube = Cube(stride)
@@ -234,19 +178,19 @@
     depth = 2 * rows
     weights = [
         Exchange(cube, held.at[at], send.at[at], receive.at[at], rows) for at in range(3)
-    ] + [Exchange(cube, output_all, send.at[3], receive.at[3], output_hbm.shape[0])]
+    ]
     loads = [
         pltpu.make_async_copy(source, weight.own, local.at[at])
         for at, (source, weight) in enumerate(
-            zip((query_hbm, key_hbm, value_hbm, output_hbm), weights)
+            zip((query_hbm, key_hbm, value_hbm), weights)
         )
     ]
-    fetch = pltpu.make_async_copy(tokens_hbm, tokens, local.at[4])
+    fetch = pltpu.make_async_copy(tokens_hbm, tokens, local.at[3])
     for load in loads:
         load.start()
     fetch.start()
     cube.barrier()
-    query, key, value, output = weights
+    query, key, value = weights
     loads[0].wait()
     query.start(2, 0, 1)
     loads[1].wait()
@@ -270,18 +214,6 @@
             else:
                 sums[at][here, :] += product
 
-    def near(weight):
-        weight.arrived(0)
-        weight.start(5, 3)
-        weight.arrived(1)
-        weight.start(6, 4)
-
-    def far(weight):
-        weight.arrived(5)
-        weight.start(7)
-        weight.arrived(6)
-        weight.start(8)
-
     def near_multiply(at):
         weights[at].arrived(3)
         multiply(at, 1)
@@ -293,67 +225,276 @@
         multiply(at, 3)
 
     loads[2].wait()
-    loads[3].wait()
     fetch.wait()
     query.arrived(2)
     multiply(0, 0)
     key.arrived(2)
     multiply(1, 0)
-    near(query)
+    query.near()
     near_multiply(0)
-    near(key)
+    key.near()
     value.start(2, 0, 1)
-    output.start(2, 0, 1)
     near_multiply(1)
     value.arrived(2)
     multiply(2, 0)
-    far(query)
+    query.far()
     far_multiply(0)
-    far(key)
+    key.far()
     far_multiply(1)
-    near(value)
+    value.near()
     near_multiply(2)
-    near(output)
-    far(value)
+    value.far()
     far_multiply(2)
     value_ref[...] = value_sum[...].astype(value_ref.dtype)
-    output.arrived(2, 3, 4)
-    far(output)
-    output.arrived(7, 8)
     for weight in weights:
         weight.sent()
 
 
-def project(tokens, query_weight, key_weight, value_weight, output_weight, stride):
+def project(tokens, query_weight, key_weight, value_weight, stride):
     count = tokens.shape[0]
     rows, width = query_weight.shape
-    output_rows, output_width = output_weight.shape
     anywhere = pl.BlockSpec(memory_space=pl.ANY)
     vmem = pl.BlockSpec(memory_space=pltpu.VMEM)
-    query, key, value, output = pl.pallas_call(
+    return pl.pallas_call(
         functools.partial(project_kernel, stride),
         out_shape=(
             jax.ShapeDtypeStruct((count, width), jnp.float32),
             jax.ShapeDtypeStruct((count, width), jnp.float32),
             jax.ShapeDtypeStruct((count, width), jnp.bfloat16),
-            jax.ShapeDtypeStruct((CUBE // 2, 2 * output_rows, output_width), jnp.bfloat16),
         ),
-        in_specs=[anywhere] * 5,
-        out_specs=(vmem, vmem, vmem, anywhere),
+        in_specs=[anywhere] * 4,
+        out_specs=(vmem, vmem, vmem),
         scratch_shapes=[
             pltpu.VMEM(tokens.shape, tokens.dtype),
             pltpu.VMEM((3, CUBE // 2, 2 * rows, width), query_weight.dtype),
             pltpu.VMEM((count, width), jnp.float32),
-            pltpu.SemaphoreType.DMA((5,)),
-            pltpu.SemaphoreType.DMA((4, 9)),
-            pltpu.SemaphoreType.DMA((4, 9)),
+            pltpu.SemaphoreType.DMA((4,)),
+            pltpu.SemaphoreType.DMA((3, 9)),
+            pltpu.SemaphoreType.DMA((3, 9)),
         ],
         compiler_params=pltpu.CompilerParams(
             collective_id=0, has_side_effects=True, vmem_limit_bytes=60 * 1024 * 1024
         ),
         name="project",
-    )(tokens, query_weight, key_weight, value_weight, output_weight)
-    return query, key, value, output.reshape(-1, output_width)
+    )(tokens, query_weight, key_weight, value_weight)
+
+
+class Line:
+    def __init__(self, blocks, send, receive):
+        self.count = lax.axis_size("head")
+        self.me = lax.axis_index("head")
+        self.blocks, self.send, self.receive = blocks, send, receive
+
+    def neighbour(self, side):
+        return self.me + 1 if side == 0 else self.me - 1
+
+    def has(self, side):
+        return self.me < self.count - 1 if side == 0 else self.me > 0
+
+    def greet(self, semaphore):
+        for side in range(2):
+            @pl.when(self.has(side))
+            def _():
+                pl.semaphore_signal(
+                    semaphore,
+                    inc=1,
+                    device_id={"head": self.neighbour(side)},
+                    device_id_type=pl.DeviceIdType.MESH,
+                )
+
+    def meet(self, semaphore, others):
+        both = self.has(0) & self.has(1)
+
+        @pl.when(both)
+        def _():
+            pl.semaphore_wait(semaphore, others + 2)
+
+        @pl.when(jnp.logical_not(both))
+        def _():
+            pl.semaphore_wait(semaphore, others + 1)
+
+    def origin(self, side, far):
+        return self.me - far if side == 0 else self.me + far
+
+    def holds(self, side, far):
+        return self.me >= far if side == 0 else self.me + far < self.count
+
+    def copy(self, side, far, at, group):
+        ref = self.blocks(group, at)
+        return pltpu.make_async_remote_copy(
+            src_ref=ref,
+            dst_ref=ref,
+            send_sem=self.send.at[side, far, at],
+            recv_sem=self.receive.at[side, far, at],
+            device_id={"head": self.neighbour(side)},
+            device_id_type=pl.DeviceIdType.MESH,
+        )
+
+    def start(self, side, far, at):
+        @pl.when(self.has(side) & self.holds(side, far))
+        def _():
+            self.copy(side, far, at, self.origin(side, far)).start()
+
+    def relay(self, far, at):
+        for side in range(2):
+            @pl.when(self.holds(side, far + 1))
+            def _():
+                self.copy(side, far, at, self.origin(side, far + 1)).wait_recv()
+
+            if far + 2 < self.count:
+                self.start(side, far + 1, at)
+
+    def sent(self, parts):
+        for side in range(2):
+            for far in range(self.count - 1):
+                @pl.when(self.has(side) & self.holds(side, far))
+                def _():
+                    @pl.loop(0, parts)
+                    def _(at):
+                        self.copy(side, far, at, self.origin(side, far)).wait_send()
+
+
+def weigh(scores, allowed):
+    scores = jnp.where(allowed, scores, -jnp.inf)
+    raised = jnp.exp(scores - jnp.max(scores, axis=-1, keepdims=True))
+    return (raised * (1.0 / jnp.sum(raised, axis=-1, keepdims=True))).astype(jnp.bfloat16)
+
+
+def score(queries, keys):
+    return lax.dot_general(
+        queries, keys, (((1,), (1,)), ((), ())), preferred_element_type=jnp.float32
+    ) * (1.0 / math.sqrt(HD))
+
+
+def attend_kernel(
+    stride, grid_columns, frames, side,
+    query_ref, key_ref, key_pad, value_pad, output_hbm,
+    result_ref,
+    spatial, mixed, held, total, local, send, receive, line_send, line_receive,
+):
+    cube = Cube(stride)
+    rows, columns = output_hbm.shape
+    weight = Exchange(cube, held, send, receive, rows)
+    load = pltpu.make_async_copy(output_hbm, weight.own, local)
+    load.start()
+    group_width = query_ref.shape[1]
+    heads_here = group_width // HD
+    tokens = query_ref.shape[0]
+
+    def head_of(at):
+        return pl.ds(pl.multiple_of(at * HD, HD), HD)
+
+    line = Line(lambda group, at: mixed.at[group, :, head_of(at)], line_send, line_receive)
+    cube.barrier(line)
+    load.wait()
+    weight.start(2, 0, 1)
+
+    area = side * side
+    wide = side + 2 * WT
+    window = wide * wide
+    place = lax.axis_index("hw")
+    tile_row = lax.div(place, grid_columns) * (side // WT) - 1
+    tile_column = lax.rem(place, grid_columns) * (side // WT) - 1
+    query_at = lax.broadcasted_iota(jnp.int32, (area, window), 0)
+    key_at = lax.broadcasted_iota(jnp.int32, (area, window), 1)
+    key_row, key_column = key_at // wide // WT, key_at % wide // WT
+    down = key_row - query_at // side // WT
+    right = key_column - query_at % side // WT
+    near = (down >= 0) & (down <= 2) & (right >= 0) & (right <= 2)
+    near &= (key_row + tile_row >= 0) & (key_row + tile_row < DEV_ROWS * (side // WT))
+    near &= (key_column + tile_column >= 0) & (
+        key_column + tile_column < grid_columns * (side // WT)
+    )
+    strip = 2 * area
+    same = (
+        lax.broadcasted_iota(jnp.int32, (strip, tokens), 0) % area
+        == lax.broadcasted_iota(jnp.int32, (strip, tokens), 1) % area
+    )
+
+    @pl.loop(0, heads_here)
+    def _(at):
+        head = head_of(at)
+        scores = [
+            score(query_ref[pl.ds(frame * area, area), head], key_pad[frame, :, head])
+            for frame in range(frames)
+        ]
+        weights = [weigh(one, near) for one in scores]
+        for frame in range(frames):
+            spatial[pl.ds(frame * area, area), :] = jnp.dot(
+                weights[frame], value_pad[frame, :, head], preferred_element_type=jnp.float32
+            ).astype(jnp.bfloat16)
+        for low in range(0, tokens, strip):
+            over = weigh(score(query_ref[pl.ds(low, strip), head], key_ref[:, head]), same)
+            mixed[line.me, pl.ds(low, strip), head] = jnp.dot(
+                over, spatial[...], preferred_element_type=jnp.float32
+            ).astype(jnp.bfloat16)
+        line.start(0, 0, at)
+        line.start(1, 0, at)
+
+    block = tokens // 2
+
+    def multiply(group, first=False):
+        @pl.loop(0, 2)
+        def _(step):
+            here = pl.ds(pl.multiple_of(step * block, block), block)
+            product = jnp.dot(mixed[group, here, :], held[group], preferred_element_type=jnp.float32)
+            if first:
+                total[here, :] = product
+            else:
+                total[here, :] += product
+
+    def relay(far):
+        @pl.loop(0, heads_here)
+        def _(at):
+            line.relay(far, at)
+
+    relay(0)
+    weight.near()
+    weight.arrived(2, 3, 4)
+    if line.count > 2:
+        relay(1)
+    weight.far()
+    weight.arrived(7, 8)
+    multiply(line.me, True)
+    for far in range(line.count - 1):
+        if far > 1:
+            relay(far)
+        for side_at in range(2):
+            @pl.when(line.holds(side_at, far + 1))
+            def _():
+                multiply(line.origin(side_at, far + 1))
+    result_ref[...] = total[...].astype(result_ref.dtype)
+    weight.sent()
+    line.sent(heads_here)
+
+
+def attend(queries, keys, key_pad, value_pad, output_weight, stride, grid_columns, frames, side):
+    tokens, group_width = queries.shape
+    rows, columns = output_weight.shape
+    groups = lax.axis_size("head")
+    heads_here = group_width // HD
+    vmem = pl.BlockSpec(memory_space=pltpu.VMEM)
+    return pl.pallas_call(
+        functools.partial(attend_kernel, stride, grid_columns, frames, side),
+        out_shape=jax.ShapeDtypeStruct((tokens, columns), jnp.bfloat16),
+        in_specs=[vmem] * 4 + [pl.BlockSpec(memory_space=pl.ANY)],
+        out_specs=vmem,
+        scratch_shapes=[
+            pltpu.VMEM((tokens, HD), jnp.bfloat16),
+            pltpu.VMEM((groups, tokens, group_width), jnp.bfloat16),
+            pltpu.VMEM((CUBE // 2, 2 * rows, columns), output_weight.dtype),
+            pltpu.VMEM((tokens, columns), jnp.float32),
+            pltpu.SemaphoreType.DMA,
+            pltpu.SemaphoreType.DMA((9,)),
+            pltpu.SemaphoreType.DMA((9,)),
+            pltpu.SemaphoreType.DMA((2, groups - 1, heads_here)),
+            pltpu.SemaphoreType.DMA((2, groups - 1, heads_here)),
+        ],
+        compiler_params=pltpu.CompilerParams(
+            collective_id=1, has_side_effects=True, vmem_limit_bytes=60 * 1024 * 1024
+        ),
+        name="attend",
+    )(queries, keys, key_pad, value_pad, output_weight)
 
 
 def pregather(weight, stride):
@@ -386,11 +527,10 @@
     place = lax.axis_index("hw")
     grid_row = place // grid_columns
     grid_column = place % grid_columns
-    tiles_side = side // WT
     stride = lax.axis_size("hw") // CUBE
-    query_lin, key_lin, values, output_all = project(
+    query_lin, key_lin, values = project(
         tokens,
-        *(pregather(w, stride) for w in (query_weight, key_weight, value_weight, output_weight)),
+        *(pregather(w, stride) for w in (query_weight, key_weight, value_weight)),
         stride,
     )
     query_squares, key_squares = lax.psum(
@@ -418,21 +558,18 @@
         for down in (-1, 0, 1)
     ]
     padded = jnp.concatenate(bands, axis=2)
-    spatial = window_attend(
-        queries_grid,
-        padded[0],
-        padded[1],
-        grid_row * tiles_side,
-        grid_column * tiles_side,
-        DEV_ROWS * tiles_side,
-        grid_columns * tiles_side,
-        heads_here,
-        head_dim,
-    )
-    mixed = frame_attend(queries_grid, keys_grid, spatial, heads_here, head_dim)
-    gathered = lax.all_gather(mixed.reshape(-1, group_width), "head", axis=1, tiled=True)
-    result = jnp.dot(gathered, output_all, preferred_element_type=jnp.float32)
-    return result.astype(jnp.bfloat16).reshape(1, frames, side, side, output_weight.shape[1])
+    result = attend(
+        queries_grid.reshape(-1, group_width),
+        keys_grid.reshape(-1, group_width),
+        padded[0].reshape(frames, -1, group_width),
+        padded[1].reshape(frames, -1, group_width),
+        pregather(output_weight, stride),
+        stride,
+        grid_columns,
+        frames,
+        side,
+    )
+    return result.reshape(1, frames, side, side, output_weight.shape[1])
 
 
 def solution(mesh):

time: 331 us -> 243 us (0.73)
  waiting for transfers between devices: 80.5 us -> 33.1 us
  Pallas kernels: 114 us -> 142 us
  local copies, waits for them, and re-layouts: 43.1 us -> 16.8 us
  matrix products: 26 us -> 3.3 us
  between operations: 14 us -> 0.34 us
  other arithmetic: 17.9 us -> 10.1 us
    all_gather x1 -> x0, waiting for transfers between devices: 53.4 us -> none  [per_device(): lax.all_gather(mixed.reshape(-1, group_width), 'head', axis=1, tiled=True)]
    pallas_call x0 -> x1, Pallas kernels: none -> 52.7 us  [attend(): pl.pallas_call(functools.partial(attend_kernel, stride, grid_columns, fra...]
    pallas_call x1, Pallas kernels: 114 us -> 89 us  [project(): pl.pallas_call(functools.partial(project_kernel, stride), out_shape=(jax....]
    dot_general x3 -> x0, matrix products: 13.3 us -> none  [the longest x1 8.26 us: per_device(): result = jnp.dot(gathered, output_all, preferred_element_type=jnp.float32)]
    another operation x3 -> x0, local copies, waits for them, and re-layouts: 11.3 us -> none  [the longest x2 11.2 us: tiles(): array.reshape(frames, across + extra, WT, along + extra, WT, heads_here,...]
    sub x2 -> x0, matrix products: 10.2 us -> none  [soft_weights(): raised = jnp.exp(scores - top)]
    transpose x4 -> x0, local copies, waits for them, and re-layouts: 8.01 us -> none  [the longest x3 7.57 us: tiles(): shaped.transpose(0, 1, 3, 2, 4, 5, 6)]
    ppermute x8, waiting for transfers between devices: 27 us -> 33.1 us  [from_behind(): lax.ppermute(value, axis, [(source, source + steps) for source in range(i...]
  transfers between devices with their start and end apart: 9 -> 8, of which waited for: 3 -> 1; matrix products, arithmetic and copies ran while one was open for 3% -> 1% of each run, Pallas kernels for 0% -> 0%
where the time goes in v2:
time: 243 us; the launch traced here: 239 us
  Pallas kernels  142 us (58%)
  waiting for transfers between devices  33.1 us (14%)
  starting transfers between devices  23.5 us (10%)
  local copies, waits for them, and re-layouts  16.8 us (7%)
  blocking collectives  10.4 us (4%)
  other arithmetic  10.1 us (4%)
  matrix products  3.3 us (1%)
    pallas_call x1, Pallas kernels, project(): pl.pallas_call(functools.partial(project_kernel, stride), out_shape=(jax....  89 us
    pallas_call x1, Pallas kernels, attend(): pl.pallas_call(functools.partial(attend_kernel, stride, grid_columns, fra...  52.7 us
    ppermute x8, waiting for transfers between devices, from_behind(): lax.ppermute(value, axis, [(source, source + steps) for source in range(i...  33.1 us
    ppermute x8, starting transfers between devices, from_behind(): lax.ppermute(value, axis, [(source, source + steps) for source in range(i...  23.5 us
    psum x1, blocking collectives, per_device(): lax.psum((jnp.sum(query_lin * query_lin, axis=1), jnp.sum(key_lin * key_l...  10.4 us
    mul x2, local copies, waits for them, and re-layouts, rotate(): rotated = shaped * cosine + turned * sine  5.57 us
  transfers between devices with their start and end apart: 8, of which 1 were waited for; matrix products, arithmetic and copies ran while one was open for 1% of the time, Pallas kernels for 0%

profile of v2, /device:TPU:5, one launch (start us, length us, event | category | flops | bytes accessed | tf_op | source)
XLA Modules:
  0.0 239.3 jit_solution(12513867748211973888)
XLA Ops:
  1.7 1.2 fusion.12
  3.6 2.2 broadcast_in_dim.13
  5.8 2.8 %copy.14 = f32[8,8,8,128]{3,2,1,0:T(8,128)S(1)} copy(f32[8,8,8,128]{2,1,3,0:T(8,128)} %bitcast.26) | data formatting | bytes 524288 | tf_op jit(solution)/shard_map/mul | solution.py:64
  9.3 2.2 broadcast_in_dim.14
  11.6 2.8 %copy.16 = f32[8,8,8,128]{3,2,1,0:T(8,128)S(1)} copy(f32[8,8,8,128]{2,1,3,0:T(8,128)} %bitcast.27) | data formatting | bytes 524288 | tf_op jit(solution)/shard_map/mul | solution.py:64
  14.4 89.0 %project.1 = (f32[512,640]{1,0:T(8,128)}, f32[512,640]{1,0:T(8,128)}, bf16[512,640]{1,0:T(8,128)(2,1)}) custom-call(bf16[512,5120]{1,0:T(8,128)(2,1)} %bitcast.34, bf16[640,640]{1,0:T(8,128)(2,1)} %query_hbm.1, bf16[640,640]{1,0:T(8,128)(2,1)} %key_hbm.1, bf16[640,640]{1,0:T(8,128)(2,1)} %value_hbm.1), custom_call_target="tpu_custom_call" | custom-call | tf_op jit(solution)/shard_map/project/pallas_call | solution.py:258
  103.4 1.6 multiply_reduce_fusion.1
  105.3 10.4 %all-reduce = (f32[512]{0:T(512)S(1)}, f32[512]{0:T(512)S(1)}) all-reduce(f32[512]{0:T(512)S(1)} %multiply_reduce_fusion.1, f32[512]{0:T(512)S(1)} %multiply_reduce_fusion), channel_id=1, replica_groups=mesh['hw'=8,'head'=4] {'head'}, use_global_device_ids=true, to_apply=%region_1.2 | all-reduce | flops 1024 | bytes 8192 | tf_op jit(solution)/shard_map/psum | solution.py:536
  116.0 1.2 fusion.3
  117.7 1.3 collective-permute-start
  119.0 3.1 %collective-permute-start.2 = (bf16[2,8,4,4,640]{4,3,2,1,0:T(4,128)(2,1)S(1)}, bf16[2,8,4,4,640]{4,3,2,1,0:T(4,128)(2,1)S(1)}, u32[]{:S(2)}, u32[]{:S(2)}) collective-permute-start(bf16[2,8,4,4,640]{4,3,2,1,0:T(4,128)(2,1)S(1)} %get-tuple-element.16), channel_id=1, source_target_pairs={{0,4},{4,8},{8,12},{12,16},{16,20},{20,24},{24,28},{1,5},{5,9},{9,... | collective-permute-start | bytes 983048 | tf_op jit(solution)/shard_map/ppermute | solution.py:23
  122.1 2.3 collective-permute-start.5
  124.5 1.9 collective-permute-start.1
  126.5 4.3 %collective-permute-start.6 = (bf16[2,8,4,8,640]{4,3,2,1,0:T(8,128)(2,1)S(1)}, bf16[2,8,4,8,640]{4,3,2,1,0:T(8,128)(2,1)S(1)}, u32[]{:S(2)}, u32[]{:S(2)}) collective-permute-start(bf16[2,8,4,8,640]{4,3,2,1,0:T(8,128)(2,1)S(1)} %get-tuple-element.20), channel_id=1, source_target_pairs={{8,0},{12,4},{16,8},{20,12},{24,16},{28,20},{9,1},{13,5},{17,9},{2... | collective-permute-start | bytes 1966088 | tf_op jit(solution)/shard_map/ppermute | solution.py:23
  130.7 0.8 fusion.6
  131.6 3.9 %collective-permute-start.3 = (bf16[2,8,8,4,640]{4,3,2,1,0:T(4,128)(2,1)S(1)}, bf16[2,8,8,4,640]{4,3,2,1,0:T(4,128)(2,1)S(1)}, u32[]{:S(2)}, u32[]{:S(2)}) collective-permute-start(bf16[2,8,8,4,640]{4,3,2,1,0:T(4,128)(2,1)S(1)} %get-tuple-element.21), channel_id=1, source_target_pairs={{0,4},{4,8},{8,12},{12,16},{16,20},{20,24},{24,28},{1,5},{5,9},{9,... | collective-permute-start | bytes 1966088 | tf_op jit(solution)/shard_map/ppermute | solution.py:23
  135.4 3.2 %collective-permute-start.4 = (bf16[2,8,8,4,640]{4,3,2,1,0:T(4,128)(2,1)S(1)}, bf16[2,8,8,4,640]{4,3,2,1,0:T(4,128)(2,1)S(1)}, u32[]{:S(2)}, u32[]{:S(2)}) collective-permute-start(bf16[2,8,8,4,640]{4,3,2,1,0:T(4,128)(2,1)S(1)} %get-tuple-element.22), channel_id=1, source_target_pairs={{4,0},{8,4},{12,8},{16,12},{20,16},{24,20},{28,24},{5,1},{9,5},{13... | collective-permute-start | bytes 1966088 | tf_op jit(solution)/shard_map/ppermute | solution.py:23
  138.6 3.6 %collective-permute-start.7 = (bf16[2,8,4,4,640]{4,3,2,1,0:T(4,128)(2,1)S(1)}, bf16[2,8,4,4,640]{4,3,2,1,0:T(4,128)(2,1)S(1)}, u32[]{:S(2)}, u32[]{:S(2)}) collective-permute-start(bf16[2,8,4,4,640]{4,3,2,1,0:T(4,128)(2,1)S(1)} %get-tuple-element.18), channel_id=1, source_target_pairs={{12,0},{16,4},{20,8},{24,12},{28,16},{13,1},{17,5},{21,9},{25,13},... | collective-permute-start | bytes 983048 | tf_op jit(solution)/shard_map/ppermute | solution.py:23
  142.2 2.1 fusion.2
  144.3 33.1 %collective-permute-done.7 = bf16[2,8,4,4,640]{4,3,2,1,0:T(4,128)(2,1)S(1)} collective-permute-done((bf16[2,8,4,4,640]{4,3,2,1,0:T(4,128)(2,1)S(1)}, bf16[2,8,4,4,640]{4,3,2,1,0:T(4,128)(2,1)S(1)}, u32[]{:S(2)}, u32[]{:S(2)}) %collective-permute-start.7) | collective-permute-done | bytes 327712 | tf_op jit(solution)/shard_map/ppermute | solution.py:23
  177.5 3.8 %maximum_maximum_fusion = bf16[2,8,16,16,640]{4,3,2,1,0:T(8,128)(2,1)S(1)} fusion(bf16[2,8,4,4,640]{4,3,2,1,0:T(4,128)(2,1)S(1)} %collective-permute-done.7, bf16[2,8,4,8,640]{4,3,2,1,0:T(8,128)(2,1)S(1)} %collective-permute-done.6, bf16[2,8,4,4,640]{4,3,2,1,0:T(4,128)(2,1)S(1)} %collective-permute-done.5, ...), kind=kLoop, calls=%fused_computation | loop fusion | flops 52428800 | bytes 10485760 | tf_op jit(solution)/shard_map/concatenate | solution.py:560
  181.3 2.8 %fusion.29 = (bf16[1,8,16,16,640]{4,3,2,1,0:T(8,128)(2,1)}, bf16[1,8,16,16,640]{4,3,2,1,0:T(8,128)(2,1)}) fusion(bf16[2,8,16,16,640]{4,3,2,1,0:T(8,128)(2,1)S(1)} %maximum_maximum_fusion), kind=kLoop, calls=%fused_computation.65 | loop fusion | bytes 10485760 | tf_op jit(solution)/shard_map/slice | solution.py:565
  184.1 52.7 %attend.1 = bf16[512,1280]{1,0:T(8,128)(2,1)} custom-call(bf16[512,640]{1,0:T(8,128)(2,1)} %bitcast.38, bf16[512,640]{1,0:T(8,128)(2,1)} %bitcast.25, bf16[8,256,640]{2,1,0:T(8,128)(2,1)} %bitcast.33, bf16[8,256,640]{2,1,0:T(8,128)(2,1)} %bitcast.32, bf16[320,1280]{1,0:T(8,128)(2,1)} %output_hbm.1), custom_call_target="tpu_custom_call" | custom-call | tf_op jit(solution)/shard_map/attend/pallas_call | solution.py:477
  236.8 2.5 %copy.19 = bf16[1,8,8,8,1280]{4,3,2,1,0:T(8,128)(2,1)} copy(bf16[1,8,8,8,1280]{4,3,2,1,0:T(8,128)(2,1)} %bitcast.37) | data formatting | bytes 2621440
  (38 shorter events, 4.2 us)
Async XLA Ops:
  103.4 1.7 copy-start.3
  103.4 12.3 %copy-start.2 = (f32[512,640]{1,0:T(8,128)S(1)}, f32[512,640]{1,0:T(8,128)}, u32[]{:S(2)}) copy-start(f32[512,640]{1,0:T(8,128)} %get-tuple-element.8) | copy-start | bytes 3932164
  103.4 12.3 %copy-start.4 = (f32[640]{0:T(1024)S(1)}, f32[640]{0:T(1024)}, u32[]{:S(2)}) copy-start(f32[640]{0:T(1024)} %param.16) | copy-start | bytes 7684
  103.4 12.2 %copy-start.5 = (f32[640]{0:T(1024)S(1)}, f32[640]{0:T(1024)}, u32[]{:S(2)}) copy-start(f32[640]{0:T(1024)} %param.15) | copy-start | bytes 7684
  116.0 1.3 copy-start.1
  117.2 60.2 %copy-start = (bf16[8,8,8,5,128]{4,2,3,1,0:T(8,128)(2,1)}, bf16[8,8,8,5,128]{4,2,3,1,0:T(8,128)(2,1)S(1)}, u32[]{:S(2)}) copy-start(bf16[8,8,8,5,128]{4,2,3,1,0:T(8,128)(2,1)S(1)} %fusion.3) | copy-start | bytes 1966084
  117.7 13.9 %collective-permute-start = (bf16[2,8,4,4,640]{4,3,2,1,0:T(4,128)(2,1)S(1)}, bf16[2,8,4,4,640]{4,3,2,1,0:T(4,128)(2,1)S(1)}, u32[]{:S(2)}, u32[]{:S(2)}) collective-permute-start(bf16[2,8,4,4,640]{4,3,2,1,0:T(4,128)(2,1)S(1)} %get-tuple-element.15), channel_id=1, source_target_pairs={{0,12},{4,16},{8,20},{12,24},{16,28},{1,13},{5,17},{9,21},{13,25},... | collective-permute-start | bytes 983048 | tf_op jit(solution)/shard_map/ppermute | solution.py:23
  119.0 16.5 %collective-permute-start.2 = (bf16[2,8,4,4,640]{4,3,2,1,0:T(4,128)(2,1)S(1)}, bf16[2,8,4,4,640]{4,3,2,1,0:T(4,128)(2,1)S(1)}, u32[]{:S(2)}, u32[]{:S(2)}) collective-permute-start(bf16[2,8,4,4,640]{4,3,2,1,0:T(4,128)(2,1)S(1)} %get-tuple-element.16), channel_id=1, source_target_pairs={{0,4},{4,8},{8,12},{12,16},{16,20},{20,24},{24,28},{1,5},{5,9},{9,... | collective-permute-start | bytes 983048 | tf_op jit(solution)/shard_map/ppermute | solution.py:23
  122.1 16.5 %collective-permute-start.5 = (bf16[2,8,4,4,640]{4,3,2,1,0:T(4,128)(2,1)S(1)}, bf16[2,8,4,4,640]{4,3,2,1,0:T(4,128)(2,1)S(1)}, u32[]{:S(2)}, u32[]{:S(2)}) collective-permute-start(bf16[2,8,4,4,640]{4,3,2,1,0:T(4,128)(2,1)S(1)} %get-tuple-element.17), channel_id=1, source_target_pairs={{4,0},{8,4},{12,8},{16,12},{20,16},{24,20},{28,24},{5,1},{9,5},{13... | collective-permute-start | bytes 983048 | tf_op jit(solution)/shard_map/ppermute | solution.py:23
  124.5 52.9 %collective-permute-start.1 = (bf16[2,8,4,8,640]{4,3,2,1,0:T(8,128)(2,1)S(1)}, bf16[2,8,4,8,640]{4,3,2,1,0:T(8,128)(2,1)S(1)}, u32[]{:S(2)}, u32[]{:S(2)}) collective-permute-start(bf16[2,8,4,8,640]{4,3,2,1,0:T(8,128)(2,1)S(1)} %get-tuple-element.19), channel_id=1, source_target_pairs={{0,8},{4,12},{8,16},{12,20},{16,24},{20,28},{1,9},{5,13},{9,17},{1... | collective-permute-start | bytes 1966088 | tf_op jit(solution)/shard_map/ppermute | solution.py:23
  126.5 51.0 %collective-permute-start.6 = (bf16[2,8,4,8,640]{4,3,2,1,0:T(8,128)(2,1)S(1)}, bf16[2,8,4,8,640]{4,3,2,1,0:T(8,128)(2,1)S(1)}, u32[]{:S(2)}, u32[]{:S(2)}) collective-permute-start(bf16[2,8,4,8,640]{4,3,2,1,0:T(8,128)(2,1)S(1)} %get-tuple-element.20), channel_id=1, source_target_pairs={{8,0},{12,4},{16,8},{20,12},{24,16},{28,20},{9,1},{13,5},{17,9},{2... | collective-permute-start | bytes 1966088 | tf_op jit(solution)/shard_map/ppermute | solution.py:23
  131.6 45.9 %collective-permute-start.3 = (bf16[2,8,8,4,640]{4,3,2,1,0:T(4,128)(2,1)S(1)}, bf16[2,8,8,4,640]{4,3,2,1,0:T(4,128)(2,1)S(1)}, u32[]{:S(2)}, u32[]{:S(2)}) collective-permute-start(bf16[2,8,8,4,640]{4,3,2,1,0:T(4,128)(2,1)S(1)} %get-tuple-element.21), channel_id=1, source_target_pairs={{0,4},{4,8},{8,12},{12,16},{16,20},{20,24},{24,28},{1,5},{5,9},{9,... | collective-permute-start | bytes 1966088 | tf_op jit(solution)/shard_map/ppermute | solution.py:23
  135.4 42.0 %collective-permute-start.4 = (bf16[2,8,8,4,640]{4,3,2,1,0:T(4,128)(2,1)S(1)}, bf16[2,8,8,4,640]{4,3,2,1,0:T(4,128)(2,1)S(1)}, u32[]{:S(2)}, u32[]{:S(2)}) collective-permute-start(bf16[2,8,8,4,640]{4,3,2,1,0:T(4,128)(2,1)S(1)} %get-tuple-element.22), channel_id=1, source_target_pairs={{4,0},{8,4},{12,8},{16,12},{20,16},{24,20},{28,24},{5,1},{9,5},{13... | collective-permute-start | bytes 1966088 | tf_op jit(solution)/shard_map/ppermute | solution.py:23
  138.6 38.8 %collective-permute-start.7 = (bf16[2,8,4,4,640]{4,3,2,1,0:T(4,128)(2,1)S(1)}, bf16[2,8,4,4,640]{4,3,2,1,0:T(4,128)(2,1)S(1)}, u32[]{:S(2)}, u32[]{:S(2)}) collective-permute-start(bf16[2,8,4,4,640]{4,3,2,1,0:T(4,128)(2,1)S(1)} %get-tuple-element.18), channel_id=1, source_target_pairs={{12,0},{16,4},{20,8},{24,12},{28,16},{13,1},{17,5},{21,9},{25,13},... | collective-permute-start | bytes 983048 | tf_op jit(solution)/shard_map/ppermute | solution.py:23

commit v3 on v2

--- a/solution.py
+++ b/solution.py
@@ -17,12 +17,6 @@
 NORM_EPS = 0.5
 
 
-def from_behind(value, axis, steps):
-    count = lax.axis_size(axis)
-    initial, last = (max(0, -steps), min(count, count - steps))
-    return lax.ppermute(value, axis, [(source, source + steps) for source in range(initial, last)])
-
-
 def freq_table(count):
     ratios = jnp.arange(count, dtype=jnp.float32) / count
     return jnp.float32(10000.0) ** (-ratios)
@@ -31,48 +25,27 @@
 def rope_angles(frame_index, row_index, column_index, head_dim):
     side_pairs = head_dim // 6
     frame_pairs = head_dim // 2 - 2 * side_pairs
-    frame_part = frame_index.astype(jnp.float32)[:, None] * freq_table(frame_pairs)[None, :]
-    row_part = row_index.astype(jnp.float32)[:, None] * freq_table(side_pairs)[None, :]
-    column_part = column_index.astype(jnp.float32)[:, None] * freq_table(side_pairs)[None, :]
-    frames, rows, columns = (frame_part.shape[0], row_part.shape[0], column_part.shape[0])
-    return jnp.concatenate(
-        [
-            jnp.broadcast_to(frame_part[:, None, None, :], (frames, rows, columns, frame_pairs)),
-            jnp.broadcast_to(row_part[None, :, None, :], (frames, rows, columns, side_pairs)),
-            jnp.broadcast_to(column_part[None, None, :, :], (frames, rows, columns, side_pairs)),
-        ],
-        axis=-1,
-    )
-
-
-def pair_turn(head_dim):
-    source = jnp.arange(head_dim)[:, None]
-    target = jnp.arange(head_dim)[None, :]
-    plus = ((target % 2 == 1) & (source == target - 1)).astype(jnp.float32)
-    minus = ((target % 2 == 0) & (source == target + 1)).astype(jnp.float32)
-    return plus - minus
-
-
-def rotate(features, angle, heads_here, head_dim):
-    frames, rows, columns = (angle.shape[0], angle.shape[1], angle.shape[2])
-    cosine = jnp.repeat(jnp.cos(angle), 2, axis=-1)[:, :, :, None, :]
-    sine = jnp.repeat(jnp.sin(angle), 2, axis=-1)[:, :, :, None, :]
-    shaped = features.reshape(frames, rows, columns, heads_here, head_dim)
-    turned = jnp.dot(
-        shaped.reshape(-1, head_dim), pair_turn(head_dim), precision=lax.Precision.HIGHEST
-    ).reshape(shaped.shape)
-    rotated = shaped * cosine + turned * sine
-    return rotated.astype(jnp.bfloat16).reshape(frames, rows, columns, heads_here * head_dim)
-
-
-def region(stack, down, right, edge):
-    rows = stack.shape[2]
-    columns = stack.shape[3]
-    row_start, row_stop = (rows - edge, rows) if down < 0 else (0, edge) if down > 0 else (0, rows)
-    column_start, column_stop = (
-        (columns - edge, columns) if right < 0 else (0, edge) if right > 0 else (0, columns)
-    )
-    return stack[:, :, row_start:row_stop, column_start:column_stop]
+
+    def lanes(before, count, after):
+        return jnp.repeat(jnp.pad(freq_table(count), (before, after)), 2)
+
+    frame_part = frame_index.astype(jnp.float32)[:, None] * lanes(0, frame_pairs, 2 * side_pairs)
+    row_part = row_index.astype(jnp.float32)[:, None] * lanes(frame_pairs, side_pairs, side_pairs)
+    column_part = column_index.astype(jnp.float32)[:, None] * lanes(
+        frame_pairs + side_pairs, side_pairs, 0
+    )
+    total = frame_part[:, None, None] + row_part[:, None] + column_part
+    return total.reshape(-1, head_dim)
+
+
+def rotate(features, cosine, sine, heads_here, head_dim):
+    even = lax.broadcasted_iota(jnp.int32, cosine.shape, 1) % 2 == 0
+    heads = []
+    for head in range(heads_here):
+        one = features[:, head * head_dim : (head + 1) * head_dim]
+        turned = jnp.where(even, -jnp.roll(one, -1, axis=1), jnp.roll(one, 1, axis=1))
+        heads.append((one * cosine + turned * sine).astype(jnp.bfloat16))
+    return jnp.concatenate(heads, axis=1)
 
 
 CUBE = 8
@@ -101,13 +74,15 @@
     def barrier(self, line=None):
         semaphore = pltpu.get_barrier_semaphore()
         if line is not None:
-            line.greet(semaphore)
+            for peers in line:
+                peers.greet(semaphore)
         for device in self.devices:
             pl.semaphore_signal(semaphore, inc=1, device_id=device, device_id_type=pl.DeviceIdType.MESH)
         if line is None:
             pl.semaphore_wait(semaphore, len(self.devices))
         else:
-            line.meet(semaphore, len(self.devices))
+            count = sum((peers.number() for peers in line), len(self.devices))
+            pl.semaphore_wait(semaphore, count)
 
 
 class Exchange:
@@ -302,16 +277,8 @@
                     device_id_type=pl.DeviceIdType.MESH,
                 )
 
-    def meet(self, semaphore, others):
-        both = self.has(0) & self.has(1)
-
-        @pl.when(both)
-        def _():
-            pl.semaphore_wait(semaphore, others + 2)
-
-        @pl.when(jnp.logical_not(both))
-        def _():
-            pl.semaphore_wait(semaphore, others + 1)
+    def number(self):
+        return ones(self.me, self.count)
 
     def origin(self, side, far):
         return self.me - far if side == 0 else self.me + far
@@ -354,6 +321,153 @@
                         self.copy(side, far, at, self.origin(side, far)).wait_send()
 
 
+def ones(me, count):
+    return 1 - lax.div(me + 1, count) + lax.div(me + count - 1, count)
+
+
+class Halo:
+    def __init__(self, sources, pads, grid_columns, side, local, send, receive, side_send, side_receive):
+        place = lax.axis_index("hw")
+        self.row, self.column = lax.div(place, grid_columns), lax.rem(place, grid_columns)
+        self.place, self.columns = place, grid_columns
+        self.sources, self.pads = sources, pads
+        self.edge, self.body = WT * side, side * side
+        self.slots = min(3, grid_columns)
+        self.own = self.column if grid_columns == 2 else self.slots // 2
+        self.local, self.send, self.receive = local, send, receive
+        self.side_send, self.side_receive = side_send, side_receive
+        self.parts = [
+            pl.ds(self.edge, self.body),
+            pl.ds(0, self.edge),
+            pl.ds(self.edge + self.body, self.edge),
+        ]
+
+    def first_column(self):
+        return 0 if self.columns == 2 else self.column - self.slots // 2
+
+    def has(self, way):
+        return [
+            self.row > 0,
+            self.row < DEV_ROWS - 1,
+            self.column > 0,
+            self.column < self.columns - 1,
+        ][way]
+
+    def device(self, way):
+        step = [-self.columns, self.columns, -1, 1][way]
+        return {"hw": self.place + step}
+
+    def greet(self, semaphore):
+        for way in range(4):
+            @pl.when(self.has(way))
+            def _():
+                pl.semaphore_signal(
+                    semaphore,
+                    inc=1,
+                    device_id=self.device(way),
+                    device_id_type=pl.DeviceIdType.MESH,
+                )
+
+    def number(self):
+        return ones(self.row, DEV_ROWS) + ones(self.column, self.columns)
+
+    def vertical(self, kind, way):
+        low = 0 if way == 0 else self.body - self.edge
+        return pltpu.make_async_remote_copy(
+            src_ref=self.sources[kind].at[:, pl.ds(low, self.edge), :],
+            dst_ref=self.pads[kind].at[self.own, :, self.parts[2 - way], :],
+            send_sem=self.send.at[kind, way],
+            recv_sem=self.receive.at[kind, way],
+            device_id=self.device(way),
+            device_id_type=pl.DeviceIdType.MESH,
+        )
+
+    def sideways(self, kind, way, part):
+        own = self.pads[kind].at[self.own, :, self.parts[part], :]
+        if self.columns == 2:
+            slot = self.own
+        else:
+            slot = self.slots - 1 if way == 2 else 0
+        return pltpu.make_async_remote_copy(
+            src_ref=self.sources[kind] if part == 0 else own,
+            dst_ref=self.pads[kind].at[slot, :, self.parts[part], :],
+            send_sem=self.side_send.at[kind, way - 2, part],
+            recv_sem=self.side_receive.at[kind, way - 2, part],
+            device_id=self.device(way),
+            device_id_type=pl.DeviceIdType.MESH,
+        )
+
+    def here(self, kind):
+        return pltpu.make_async_copy(
+            self.sources[kind],
+            self.pads[kind].at[self.own, :, self.parts[0], :],
+            self.local.at[kind],
+        )
+
+    def start(self):
+        for kind in range(2):
+            self.here(kind).start()
+        for kind in range(2):
+            for way in range(2):
+                @pl.when(self.has(way))
+                def _():
+                    self.vertical(kind, way).start()
+            for way in (2, 3):
+                @pl.when(self.has(way))
+                def _():
+                    self.sideways(kind, way, 0).start()
+        for pad in self.pads:
+            for way in range(2):
+                @pl.when(jnp.logical_not(self.has(way)))
+                def _():
+                    for slot in range(self.slots):
+                        place = pad.at[slot, :, self.parts[1 + way], :]
+                        place[...] = jnp.zeros(place.shape, pad.dtype)
+
+            if self.columns > 2:
+                for way in (2, 3):
+                    @pl.when(jnp.logical_not(self.has(way)))
+                    def _():
+                        place = pad.at[0 if way == 2 else self.slots - 1]
+                        place[...] = jnp.zeros(place.shape, pad.dtype)
+
+    def finish(self):
+        for kind in range(2):
+            for came in range(2):
+                @pl.when(self.has(came))
+                def _():
+                    self.vertical(kind, 1 - came).wait_recv()
+                    for way in (2, 3):
+                        @pl.when(self.has(way))
+                        def _():
+                            self.sideways(kind, way, 1 + came).start()
+        for kind in range(2):
+            self.here(kind).wait()
+            for came in (2, 3):
+                @pl.when(self.has(came))
+                def _():
+                    self.sideways(kind, 5 - came, 0).wait_recv()
+                    for part in range(2):
+                        @pl.when(self.has(part))
+                        def _():
+                            self.sideways(kind, 5 - came, 1 + part).wait_recv()
+
+    def sent(self):
+        for kind in range(2):
+            for way in range(2):
+                @pl.when(self.has(way))
+                def _():
+                    self.vertical(kind, way).wait_send()
+            for way in (2, 3):
+                @pl.when(self.has(way))
+                def _():
+                    self.sideways(kind, way, 0).wait_send()
+                    for part in range(2):
+                        @pl.when(self.has(part))
+                        def _():
+                            self.sideways(kind, way, 1 + part).wait_send()
+
+
 def weigh(scores, allowed):
     scores = jnp.where(allowed, scores, -jnp.inf)
     raised = jnp.exp(scores - jnp.max(scores, axis=-1, keepdims=True))
@@ -368,9 +482,10 @@
 
 def attend_kernel(
     stride, grid_columns, frames, side,
-    query_ref, key_ref, key_pad, value_pad, output_hbm,
+    query_ref, key_ref, value_ref, output_hbm,
     result_ref,
-    spatial, mixed, held, total, local, send, receive, line_send, line_receive,
+    key_pad, value_pad, spatial, mixed, held, total, local, send, receive, line_send, line_receive,
+    halo_local, halo_send, halo_receive, side_send, side_receive,
 ):
     cube = Cube(stride)
     rows, columns = output_hbm.shape
@@ -385,46 +500,55 @@
         return pl.ds(pl.multiple_of(at * HD, HD), HD)
 
     line = Line(lambda group, at: mixed.at[group, :, head_of(at)], line_send, line_receive)
-    cube.barrier(line)
+    halo = Halo(
+        (key_ref, value_ref), (key_pad, value_pad), grid_columns, side,
+        halo_local, halo_send, halo_receive, side_send, side_receive,
+    )
+    cube.barrier((line, halo))
+    halo.start()
     load.wait()
     weight.start(2, 0, 1)
 
     area = side * side
-    wide = side + 2 * WT
-    window = wide * wide
-    place = lax.axis_index("hw")
-    tile_row = lax.div(place, grid_columns) * (side // WT) - 1
-    tile_column = lax.rem(place, grid_columns) * (side // WT) - 1
-    query_at = lax.broadcasted_iota(jnp.int32, (area, window), 0)
-    key_at = lax.broadcasted_iota(jnp.int32, (area, window), 1)
-    key_row, key_column = key_at // wide // WT, key_at % wide // WT
-    down = key_row - query_at // side // WT
-    right = key_column - query_at % side // WT
-    near = (down >= 0) & (down <= 2) & (right >= 0) & (right <= 2)
-    near &= (key_row + tile_row >= 0) & (key_row + tile_row < DEV_ROWS * (side // WT))
-    near &= (key_column + tile_column >= 0) & (
-        key_column + tile_column < grid_columns * (side // WT)
-    )
+    tall = side + 2 * WT
+    window = tall * side
+    keys_here = halo.slots * window
+    tiles = side // WT
+    query_at = lax.broadcasted_iota(jnp.int32, (area, keys_here), 0)
+    key_at = lax.broadcasted_iota(jnp.int32, (area, keys_here), 1)
+    key_row = halo.row * tiles - 1 + key_at % window // side // WT
+    key_column = (halo.first_column() + key_at // window) * tiles + key_at % side // WT
+    down = key_row - halo.row * tiles - query_at // side // WT
+    right = key_column - halo.column * tiles - query_at % side // WT
+    near = (down >= -1) & (down <= 1) & (right >= -1) & (right <= 1)
+    near &= (key_row >= 0) & (key_row < DEV_ROWS * tiles)
+    near &= (key_column >= 0) & (key_column < grid_columns * tiles)
     strip = 2 * area
     same = (
         lax.broadcasted_iota(jnp.int32, (strip, tokens), 0) % area
         == lax.broadcasted_iota(jnp.int32, (strip, tokens), 1) % area
     )
 
+    halo.finish()
+
+    def window_of(pad, frame, head):
+        return jnp.concatenate([pad[slot, frame, :, head] for slot in range(halo.slots)], axis=0)
+
     @pl.loop(0, heads_here)
     def _(at):
         head = head_of(at)
+        own_keys = key_ref[:, :, head].reshape(tokens, HD)
         scores = [
-            score(query_ref[pl.ds(frame * area, area), head], key_pad[frame, :, head])
+            score(query_ref[pl.ds(frame * area, area), head], window_of(key_pad, frame, head))
             for frame in range(frames)
         ]
         weights = [weigh(one, near) for one in scores]
         for frame in range(frames):
             spatial[pl.ds(frame * area, area), :] = jnp.dot(
-                weights[frame], value_pad[frame, :, head], preferred_element_type=jnp.float32
+                weights[frame], window_of(value_pad, frame, head), preferred_element_type=jnp.float32
             ).astype(jnp.bfloat16)
         for low in range(0, tokens, strip):
-            over = weigh(score(query_ref[pl.ds(low, strip), head], key_ref[:, head]), same)
+            over = weigh(score(query_ref[pl.ds(low, strip), head], own_keys), same)
             mixed[line.me, pl.ds(low, strip), head] = jnp.dot(
                 over, spatial[...], preferred_element_type=jnp.float32
             ).astype(jnp.bfloat16)
@@ -466,20 +590,26 @@
     result_ref[...] = total[...].astype(result_ref.dtype)
     weight.sent()
     line.sent(heads_here)
-
-
-def attend(queries, keys, key_pad, value_pad, output_weight, stride, grid_columns, frames, side):
+    halo.sent()
+
+
+def attend(queries, keys, values, output_weight, stride, grid_columns, frames, side):
     tokens, group_width = queries.shape
     rows, columns = output_weight.shape
     groups = lax.axis_size("head")
+    pad = pltpu.VMEM(
+        (min(3, grid_columns), frames, side * (side + 2 * WT), group_width), jnp.bfloat16
+    )
     heads_here = group_width // HD
     vmem = pl.BlockSpec(memory_space=pltpu.VMEM)
     return pl.pallas_call(
         functools.partial(attend_kernel, stride, grid_columns, frames, side),
         out_shape=jax.ShapeDtypeStruct((tokens, columns), jnp.bfloat16),
-        in_specs=[vmem] * 4 + [pl.BlockSpec(memory_space=pl.ANY)],
+        in_specs=[vmem] * 3 + [pl.BlockSpec(memory_space=pl.ANY)],
         out_specs=vmem,
         scratch_shapes=[
+            pad,
+            pad,
             pltpu.VMEM((tokens, HD), jnp.bfloat16),
             pltpu.VMEM((groups, tokens, group_width), jnp.bfloat16),
             pltpu.VMEM((CUBE // 2, 2 * rows, columns), output_weight.dtype),
@@ -489,12 +619,17 @@
             pltpu.SemaphoreType.DMA((9,)),
             pltpu.SemaphoreType.DMA((2, groups - 1, heads_here)),
             pltpu.SemaphoreType.DMA((2, groups - 1, heads_here)),
+            pltpu.SemaphoreType.DMA((2,)),
+            pltpu.SemaphoreType.DMA((2, 2)),
+            pltpu.SemaphoreType.DMA((2, 2)),
+            pltpu.SemaphoreType.DMA((2, 2, 3)),
+            pltpu.SemaphoreType.DMA((2, 2, 3)),
         ],
         compiler_params=pltpu.CompilerParams(
             collective_id=1, has_side_effects=True, vmem_limit_bytes=60 * 1024 * 1024
         ),
         name="attend",
-    )(queries, keys, key_pad, value_pad, output_weight)
+    )(queries, keys, values, output_weight)
 
 
 def pregather(weight, stride):
@@ -541,28 +676,13 @@
     rows_here = lax.dynamic_slice_in_dim(row_index, grid_row * side, side)
     columns_here = lax.dynamic_slice_in_dim(column_index, grid_column * side, side)
     angle = rope_angles(frame_index, rows_here, columns_here, head_dim)
-    queries_grid = rotate(query_norm, angle, heads_here, head_dim)
-    keys_grid = rotate(key_norm, angle, heads_here, head_dim)
-    values_grid = values.reshape(frames, side, side, group_width)
-    stack = jnp.stack([keys_grid, values_grid])
-    received = {}
-    for down in (-1, 0, 1):
-        for right in (-1, 0, 1):
-            if down != 0 or right != 0:
-                received[down, right] = from_behind(
-                    region(stack, down, right, WT), "hw", -(down * grid_columns + right)
-                )
-    received[0, 0] = stack
-    bands = [
-        jnp.concatenate([received[down, right] for right in (-1, 0, 1)], axis=3)
-        for down in (-1, 0, 1)
-    ]
-    padded = jnp.concatenate(bands, axis=2)
+    cosine, sine = jnp.cos(angle), jnp.sin(angle)
+    queries = rotate(query_norm, cosine, sine, heads_here, head_dim)
+    keys = rotate(key_norm, cosine, sine, heads_here, head_dim)
     result = attend(
-        queries_grid.reshape(-1, group_width),
-        keys_grid.reshape(-1, group_width),
-        padded[0].reshape(frames, -1, group_width),
-        padded[1].reshape(frames, -1, group_width),
+        queries,
+        keys.reshape(frames, -1, group_width),
+        values.reshape(frames, -1, group_width),
         pregather(output_weight, stride),
         stride,
         grid_columns,

time: 243 us -> 198 us (0.81); the launches traced: 239 us -> 197 us
  waiting for transfers between devices: 33.1 us -> 0 us
  Pallas kernels: 142 us -> 173 us
  starting transfers between devices: 23.5 us -> 0 us
  local copies, waits for them, and re-layouts: 16.8 us -> 6.73 us
  matrix products: 3.3 us -> 0 us
  other arithmetic: 10.1 us -> 7.08 us
    ppermute x8 -> x0, waiting for transfers between devices: 33.1 us -> none  [from_behind(): lax.ppermute(value, axis, [(source, source + steps) for source in range(i...]
    pallas_call x1, Pallas kernels: 52.7 us -> 83.9 us  [attend(): pl.pallas_call(functools.partial(attend_kernel, stride, grid_columns, fra...]
    ppermute x8 -> x0, starting transfers between devices: 23.5 us -> none  [from_behind(): lax.ppermute(value, axis, [(source, source + steps) for source in range(i...]
    mul x2 -> x3, local copies, waits for them, and re-layouts: 5.57 us -> 0.44 us  [the longest x1 0.15 us: rope_angles(): row_index.astype(jnp.float32)[:, None]]
    broadcast_in_dim x5 -> x3, local copies, waits for them, and re-layouts: 4.55 us -> 0.21 us  [lanes(): return jnp.repeat(jnp.pad(freq_table(count), (before, after)), 2)]
    concatenate x1 -> x0, other arithmetic: 3.82 us -> none  [per_device(): padded = jnp.concatenate(bands, axis=2)]
    dot_general x2 -> x0, matrix products: 3.3 us -> none  [rotate(): jnp.dot(shaped.reshape(-1, head_dim), pair_turn(head_dim), precision=lax....]
    convert_element_type x2 -> x8, other arithmetic: 1.41 us -> 3.89 us  [the longest x5 1.77 us: rotate(): heads.append((one * cosine + turned * sine).astype(jnp.bfloat16))]
  transfers between devices with their start and end apart: 8 -> 0, of which waited for: 1 -> 0; matrix products, arithmetic and copies ran while one was open for 1% -> 0% of each run, Pallas kernels for 0% -> 0%
where the time goes in v3:
time: 198 us; the launch traced here: 197 us
  Pallas kernels  173 us (87%)
  blocking collectives  10.4 us (5%)
  other arithmetic  7.08 us (4%)
  local copies, waits for them, and re-layouts  6.73 us (3%)
    pallas_call x1, Pallas kernels, project(): pl.pallas_call(functools.partial(project_kernel, stride), out_shape=(jax....  89 us
    pallas_call x1, Pallas kernels, attend(): pl.pallas_call(functools.partial(attend_kernel, stride, grid_columns, fra...  83.9 us
    psum x1, blocking collectives, per_device(): lax.psum((jnp.sum(query_lin * query_lin, axis=1), jnp.sum(key_lin * key_l...  10.4 us
    unnamed x21, local copies, waits for them, and re-layouts  4.24 us

profile of v3, /device:TPU:5, one launch (start us, length us, event | category | flops | bytes accessed | tf_op | source)
XLA Modules:
  0.0 197.4 jit_solution(13876056820181092624)
XLA Ops:
  0.0 0.7 dynamic-slice_convert_fusion
  0.7 0.7 dynamic-slice_convert_fusion.1
  1.5 0.7 convert_element_type.45
  2.3 0.2 mul.172
  2.8 0.1 mul.177
  3.1 0.9 add_cosine_fusion
  4.0 89.0 %project.1 = (f32[512,640]{1,0:T(8,128)}, f32[512,640]{1,0:T(8,128)}, bf16[512,640]{1,0:T(8,128)(2,1)}) custom-call(bf16[512,5120]{1,0:T(8,128)(2,1)} %bitcast.27, bf16[640,640]{1,0:T(8,128)(2,1)} %query_hbm.1, bf16[640,640]{1,0:T(8,128)(2,1)} %key_hbm.1, bf16[640,640]{1,0:T(8,128)(2,1)} %value_hbm.1), custom_call_target="tpu_custom_call" | custom-call | tf_op jit(solution)/shard_map/project/pallas_call | solution.py:233
  93.0 1.6 multiply_reduce_fusion.1
  94.7 0.2 multiply_reduce_fusion
  94.9 10.4 %all-reduce.3 = (f32[512]{0:T(512)S(1)}, f32[512]{0:T(512)S(1)}) all-reduce(f32[512]{0:T(512)S(1)} %multiply_reduce_fusion.1, f32[512]{0:T(512)S(1)} %multiply_reduce_fusion), channel_id=1, replica_groups=mesh['hw'=8,'head'=4] {'head'}, use_global_device_ids=true, to_apply=%region_1.2 | all-reduce | flops 1024 | bytes 8192 | tf_op jit(solution)/shard_map/psum | solution.py:671
  105.3 0.3 multiply_multiply_fusion
  105.6 0.4 fusion.41
  106.0 0.4 fusion.40
  106.4 0.4 fusion.5
  106.8 0.4 fusion.1
  107.2 0.4 fusion.43
  107.6 0.4 fusion.42
  108.0 0.4 fusion.9
  108.4 0.4 fusion.15
  108.7 0.4 fusion.11
  109.5 0.6 copy-done.2
  110.1 0.8 copy-done.3
  111.0 83.9 %attend.1 = bf16[512,1280]{1,0:T(8,128)(2,1)} custom-call(bf16[512,640]{1,0:T(8,128)(2,1)} %copy-done.3, bf16[8,64,640]{2,1,0:T(8,128)(2,1)} %bitcast.28, bf16[8,64,640]{2,1,0:T(8,128)(2,1)} %bitcast.29, bf16[320,1280]{1,0:T(8,128)(2,1)} %output_hbm.1), custom_call_target="tpu_custom_call" | custom-call | tf_op jit(solution)/shard_map/attend/pallas_call | solution.py:605
  194.9 2.5 %copy.20 = bf16[1,8,8,8,1280]{4,3,2,1,0:T(8,128)(2,1)} copy(bf16[1,8,8,8,1280]{4,3,2,1,0:T(8,128)(2,1)} %bitcast.26) | data formatting | bytes 2621440
  (35 shorter events, 1.0 us)
Async XLA Ops:
  93.0 1.7 copy-start.1
  93.0 12.3 %copy-start = (f32[512,640]{1,0:T(8,128)S(1)}, f32[512,640]{1,0:T(8,128)}, u32[]{:S(2)}) copy-start(f32[512,640]{1,0:T(8,128)} %get-tuple-element.8) | copy-start | bytes 3932164
  93.0 12.3 %copy-start.4 = (f32[640]{0:T(1024)S(1)}, f32[640]{0:T(1024)}, u32[]{:S(2)}) copy-start(f32[640]{0:T(1024)} %param.16) | copy-start | bytes 7684
  93.0 12.2 %copy-start.5 = (f32[640]{0:T(1024)S(1)}, f32[640]{0:T(1024)}, u32[]{:S(2)}) copy-start(f32[640]{0:T(1024)} %param.15) | copy-start | bytes 7684
  109.3 0.8 copy-start.2
  110.1 0.8 copy-start.3

commit v4 on v3

--- a/solution.py
+++ b/solution.py
@@ -143,10 +143,55 @@
             one.wait_send()
 
 
+class Peers:
+    def __init__(self, parts, send, receive):
+        self.count = lax.axis_size("head")
+        self.me = lax.axis_index("head")
+        self.parts, self.send, self.receive = parts, send, receive
+
+    def device(self, step):
+        return {"head": lax.rem(self.me + step, self.count)}
+
+    def greet(self, semaphore):
+        for step in range(1, self.count):
+            pl.semaphore_signal(
+                semaphore,
+                inc=1,
+                device_id=self.device(step),
+                device_id_type=pl.DeviceIdType.MESH,
+            )
+
+    def number(self):
+        return self.count - 1
+
+    def copy(self, step, group):
+        ref = self.parts.at[group]
+        return pltpu.make_async_remote_copy(
+            src_ref=ref,
+            dst_ref=ref,
+            send_sem=self.send.at[step - 1],
+            recv_sem=self.receive.at[step - 1],
+            device_id=self.device(step),
+            device_id_type=pl.DeviceIdType.MESH,
+        )
+
+    def start(self):
+        for step in range(1, self.count):
+            self.copy(step, self.me).start()
+
+    def finish(self):
+        for step in range(1, self.count):
+            self.copy(step, lax.rem(self.me + self.count - step, self.count)).wait_recv()
+
+    def sent(self):
+        for step in range(1, self.count):
+            self.copy(step, self.me).wait_send()
+
+
 def project_kernel(
     stride, tokens_hbm, query_hbm, key_hbm, value_hbm,
-    query_ref, key_ref, value_ref,
-    tokens, held, value_sum, local, send, receive,
+    query_ref, key_ref, value_ref, squares_ref,
+    tokens, held, value_sum, parts, local, send, receive, parts_send, parts_receive,
 ):
     cube = Cube(stride)
     rows = query_hbm.shape[0]
@@ -164,7 +209,8 @@
     for load in loads:
         load.start()
     fetch.start()
-    cube.barrier()
+    peers = Peers(parts, parts_send, parts_receive)
+    cube.barrier((peers,))
     query, key, value = weights
     loads[0].wait()
     query.start(2, 0, 1)
@@ -216,11 +262,24 @@
     far_multiply(0)
     key.far()
     far_multiply(1)
+    for at in range(2):
+        lin = sums[at][...]
+        parts[peers.me, at] = lax.dot_general(
+            jnp.ones((8, lin.shape[1]), jnp.float32),
+            lin * lin,
+            (((1,), (1,)), ((), ())),
+            precision=lax.Precision.HIGHEST,
+            preferred_element_type=jnp.float32,
+        )
+    peers.start()
     value.near()
     near_multiply(2)
     value.far()
     far_multiply(2)
     value_ref[...] = value_sum[...].astype(value_ref.dtype)
+    peers.finish()
+    squares_ref[...] = sum(parts[group] for group in range(peers.count))
+    peers.sent()
     for weight in weights:
         weight.sent()
 
@@ -228,6 +287,7 @@
 def project(tokens, query_weight, key_weight, value_weight, stride):
     count = tokens.shape[0]
     rows, width = query_weight.shape
+    groups = lax.axis_size("head")
     anywhere = pl.BlockSpec(memory_space=pl.ANY)
     vmem = pl.BlockSpec(memory_space=pltpu.VMEM)
     return pl.pallas_call(
@@ -236,16 +296,20 @@
             jax.ShapeDtypeStruct((count, width), jnp.float32),
             jax.ShapeDtypeStruct((count, width), jnp.float32),
             jax.ShapeDtypeStruct((count, width), jnp.bfloat16),
+            jax.ShapeDtypeStruct((2, 8, count), jnp.float32),
         ),
         in_specs=[anywhere] * 4,
-        out_specs=(vmem, vmem, vmem),
+        out_specs=(vmem, vmem, vmem, vmem),
         scratch_shapes=[
             pltpu.VMEM(tokens.shape, tokens.dtype),
             pltpu.VMEM((3, CUBE // 2, 2 * rows, width), query_weight.dtype),
             pltpu.VMEM((count, width), jnp.float32),
+            pltpu.VMEM((groups, 2, 8, count), jnp.float32),
             pltpu.SemaphoreType.DMA((4,)),
             pltpu.SemaphoreType.DMA((3, 9)),
             pltpu.SemaphoreType.DMA((3, 9)),
+            pltpu.SemaphoreType.DMA((groups - 1,)),
+            pltpu.SemaphoreType.DMA((groups - 1,)),
         ],
         compiler_params=pltpu.CompilerParams(
             collective_id=0, has_side_effects=True, vmem_limit_bytes=60 * 1024 * 1024
@@ -507,7 +571,6 @@
     cube.barrier((line, halo))
     halo.start()
     load.wait()
-    weight.start(2, 0, 1)
 
     area = side * side
     tall = side + 2 * WT
@@ -530,6 +593,7 @@
     )
 
     halo.finish()
+    weight.start(2, 0, 1)
 
     def window_of(pad, frame, head):
         return jnp.concatenate([pad[slot, frame, :, head] for slot in range(halo.slots)], axis=0)
@@ -663,14 +727,12 @@
     grid_row = place // grid_columns
     grid_column = place % grid_columns
     stride = lax.axis_size("hw") // CUBE
-    query_lin, key_lin, values = project(
+    query_lin, key_lin, values, squares = project(
         tokens,
         *(pregather(w, stride) for w in (query_weight, key_weight, value_weight)),
         stride,
     )
-    query_squares, key_squares = lax.psum(
-        (jnp.sum(query_lin * query_lin, axis=1), jnp.sum(key_lin * key_lin, axis=1)), "head"
-    )
+    query_squares, key_squares = squares[0, 0], squares[1, 0]
     query_norm = query_lin * lax.rsqrt(query_squares / full_width + NORM_EPS)[:, None] * query_gain
     key_norm = key_lin * lax.rsqrt(key_squares / full_width + NORM_EPS)[:, None] * key_gain
     rows_here = lax.dynamic_slice_in_dim(row_index, grid_row * side, side)

time: 198 us -> 190 us (0.960)
  blocking collectives: 10.4 us -> 0 us
    psum x1 -> x0, blocking collectives: 10.4 us -> none  [per_device(): lax.psum((jnp.sum(query_lin * query_lin, axis=1), jnp.sum(key_lin * key_l...]
    pallas_call x1, Pallas kernels: 89 us -> 91.3 us  [project(): pl.pallas_call(functools.partial(project_kernel, stride), out_shape=(jax....]
    unnamed x21 -> x17, local copies, waits for them, and re-layouts: 4.24 us -> 4.2 us
where the time goes in v4:
time: 190 us; the launch traced here: 189 us
  Pallas kernels  174 us (92%)
  other arithmetic  7.73 us (4%)
  local copies, waits for them, and re-layouts  6.68 us (4%)
    pallas_call x1, Pallas kernels, project(): pl.pallas_call(functools.partial(project_kernel, stride), out_shape=(jax....  91.3 us
    pallas_call x1, Pallas kernels, attend(): pl.pallas_call(functools.partial(attend_kernel, stride, grid_columns, fra...  83 us
    unnamed x17, local copies, waits for them, and re-layouts  4.2 us

profile of v4, /device:TPU:5, one launch (start us, length us, event | category | flops | bytes accessed | tf_op | source)
XLA Modules:
  0.0 189.0 jit_solution(799688787486551747)
XLA Ops:
  0.0 0.7 dynamic-slice_convert_fusion
  0.7 0.7 dynamic-slice_convert_fusion.1
  1.5 0.7 convert_element_type.45
  2.1 0.1 fusion.44
  2.3 0.2 mul.165
  2.5 0.1 mul.160
  2.8 0.1 mul.170
  3.1 0.9 add_cosine_fusion
  4.0 91.3 %project.1 = (f32[512,640]{1,0:T(8,128)}, f32[512,640]{1,0:T(8,128)}, bf16[512,640]{1,0:T(8,128)(2,1)}, f32[2,8,512]{2,1,0:T(8,128)}) custom-call(bf16[512,5120]{1,0:T(8,128)(2,1)} %bitcast.29, bf16[640,640]{1,0:T(8,128)(2,1)} %query_hbm.1, bf16[640,640]{1,0:T(8,128)(2,1)} %key_hbm.1, bf16[640,640]{1,0:T(8,128)(2,1)} %value_hbm.1), custom_call_target="tpu_custom_call" | custom-call | tf_op jit(solution)/shard_map/project/pallas_call | solution.py:293
  95.4 0.7 add_rsqrt_fusion
  96.1 2.0 %multiply_multiply_fusion = (f32[512,640]{1,0:T(8,128)S(1)}, f32[512,640]{1,0:T(8,128)S(1)}) fusion(f32[512,640]{1,0:T(8,128)} %get-tuple-element.11, f32[640]{0:T(1024)S(1)} %copy-done.2, f32[512]{0:T(512)S(1)} %bitcast.32, f32[640]{0:T(1024)S(1)} %copy-done.3, f32[512,640]{1,0:T(8,128)} %get-tuple-element.9, f32[512]{0:T(512)S(1)} %bitcast.33), kind=kLoop, calls=%fused_computation | loop fusion | flops 1310720 | bytes 5252096 | tf_op jit(solution)/shard_map/mul | solution.py:737
  98.1 0.4 fusion.41
  98.6 0.4 fusion.40
  99.0 0.4 fusion.5
  99.4 0.4 fusion.1
  99.7 0.4 fusion.43
  100.1 0.4 fusion.42
  100.6 0.4 fusion.9
  100.9 0.4 fusion.15
  101.3 0.4 fusion.11
  102.0 0.6 copy-done
  102.7 0.8 copy-done.1
  103.5 83.0 %attend.1 = bf16[512,1280]{1,0:T(8,128)(2,1)} custom-call(bf16[512,640]{1,0:T(8,128)(2,1)} %copy-done.1, bf16[8,64,640]{2,1,0:T(8,128)(2,1)} %bitcast.30, bf16[8,64,640]{2,1,0:T(8,128)(2,1)} %bitcast.31, bf16[320,1280]{1,0:T(8,128)(2,1)} %output_hbm.1), custom_call_target="tpu_custom_call" | custom-call | tf_op jit(solution)/shard_map/attend/pallas_call | solution.py:669
  186.6 2.5 %copy.20 = bf16[1,8,8,8,1280]{4,3,2,1,0:T(8,128)(2,1)} copy(bf16[1,8,8,8,1280]{4,3,2,1,0:T(8,128)(2,1)} %bitcast.28) | data formatting | bytes 2621440
  (27 shorter events, 0.7 us)
Async XLA Ops:
  4.0 92.1 %copy-start.2 = (f32[640]{0:T(1024)S(1)}, f32[640]{0:T(1024)}, u32[]{:S(2)}) copy-start(f32[640]{0:T(1024)} %param.16) | copy-start | bytes 7684
  4.0 92.1 %copy-start.3 = (f32[640]{0:T(1024)S(1)}, f32[640]{0:T(1024)}, u32[]{:S(2)}) copy-start(f32[640]{0:T(1024)} %param.15) | copy-start | bytes 7684
  101.8 0.8 copy-start
  102.7 0.8 copy-start.1
